TPU v7x, 256 devices: a whole 4x4x8 slice. The times are simulated.
256 devices in a mesh: boxes: 256 (over z, x, y, core).
Axes of the slice: x: 4, y: 4, z: 8, core: 2. Of those that a mesh axis runs over, the one named last changes fastest.
Arguments:
- conserved: float32 [256, 5, 16, 32, 128], P('boxes'), may hold values from -6 to 6
- volume_fraction: float32 [256, 16, 32, 128], P('boxes'), may hold values from 0.05 to 1
- cut_mask: int32 [256, 16, 32, 128], P('boxes'), may hold values 0 or 1
- merge_code: int32 [256, 16, 32, 128], P('boxes'), may hold values from 0 to 26
Outputs:
- redistributed: float32 [256, 5, 16, 32, 128], P('boxes')
All inputs are finite; a program needn't handle non-finite values. No bound on the sum of `cut_mask` on one device may be relied on, other than what follows from the above.
Results may differ from a plain program's by a relative error of at most 0.0003.
Values sent between devices are 32-bit elements; how exact they have to be, the bound alone decides.
A program may use at most 64 MiB of HBM per device.

v0:
```python
import jax
import jax.numpy as jnp
from jax import lax
from jax.sharding import PartitionSpec as P

NBY = 4
NBZ = 4


OFFSETS = [
    (first, second, third)
    for first in (-1, 0, 1)
    for second in (-1, 0, 1)
    for third in (-1, 0, 1)
    if (first, second, third) != (0, 0, 0)
]


def shifted(shard, axis, by):
    devices = lax.axis_size(axis)
    pairs = [(i, i + by) for i in range(devices) if 0 <= i + by < devices]
    return lax.ppermute(shard, axis, pairs)


def decode(code_field):
    sign_parts = (code_field // 9 - 1, code_field // 3 % 3 - 1, code_field % 3 - 1)
    members = []
    for offset in OFFSETS:
        inside = jnp.ones(code_field.shape, jnp.bool_)
        for direction, component in zip(sign_parts, offset):
            if component != 0:
                inside = inside & (direction == component)
        members.append(inside)
    return members


def placed(values, offset):
    spread = [(0, 0)] * (values.ndim - 3) + [(1 + component, 1 - component) for component in offset]
    return jnp.pad(values, spread)


def count_members(members):
    running = placed(jnp.ones(members[0].shape, jnp.float32), (0, 0, 0))
    for offset, inside in zip(OFFSETS, members):
        running = running + placed(inside.astype(jnp.float32), offset)
    return running


def window(weighted, offset, interior):
    starts = [0] + [1 + component for component in offset]
    limits = [weighted.shape[0]] + [anchor + extent for anchor, extent in zip(starts[1:], interior)]
    return lax.slice(weighted, starts, limits)


def neighbour_average(weighted, members):
    interior = [extent - 2 for extent in weighted.shape[1:]]
    running = window(weighted, (0, 0, 0), interior)
    for offset, inside in zip(OFFSETS, members):
        running = running + jnp.where(inside[None], window(weighted, offset, interior), 0.0)
    return running[1:] / running[0:1]


def spread_back(average, members):
    running = placed(average, (0, 0, 0))
    for offset, inside in zip(OFFSETS, members):
        running = running + placed(jnp.where(inside[None], average, 0.0), offset)
    return running


def exchange_rims(values, spatial_dim, stride, layers, low_edge, high_edge):
    extent = values.shape[spatial_dim]
    lower_rim = lax.slice_in_dim(values, 0, layers, axis=spatial_dim)
    upper_rim = lax.slice_in_dim(values, extent - layers, extent, axis=spatial_dim)
    from_below = shifted(upper_rim, "boxes", stride)
    from_above = shifted(lower_rim, "boxes", -stride)
    from_below = jnp.where(low_edge, 0.0, from_below)
    from_above = jnp.where(high_edge, 0.0, from_above)
    return jnp.concatenate([from_below, values, from_above], axis=spatial_dim)


def fill_ghosts(values, layers, edges):
    strides = (NBY * NBZ, NBZ, 1)
    for spatial_dim in (3, 2, 1):
        low_edge, high_edge = edges[spatial_dim - 1]
        values = exchange_rims(
            values, spatial_dim, strides[spatial_dim - 1], layers, low_edge, high_edge
        )
    return values


def return_rims(values, spatial_dim, stride, low_edge, high_edge):
    extent = values.shape[spatial_dim]
    lower_ghost = lax.slice_in_dim(values, 0, 1, axis=spatial_dim)
    upper_ghost = lax.slice_in_dim(values, extent - 1, extent, axis=spatial_dim)
    from_below = shifted(upper_ghost, "boxes", stride)
    from_above = shifted(lower_ghost, "boxes", -stride)
    from_below = jnp.where(low_edge, 0.0, from_below)
    from_above = jnp.where(high_edge, 0.0, from_above)
    leading = lax.slice_in_dim(values, 1, 2, axis=spatial_dim) + from_below
    middle = lax.slice_in_dim(values, 2, extent - 2, axis=spatial_dim)
    trailing = lax.slice_in_dim(values, extent - 2, extent - 1, axis=spatial_dim) + from_above
    return jnp.concatenate([leading, middle, trailing], axis=spatial_dim)


def sum_ghosts(values, edges):
    strides = (NBY * NBZ, NBZ, 1)
    for spatial_dim in (1, 2, 3):
        low_edge, high_edge = edges[spatial_dim - 1]
        values = return_rims(values, spatial_dim, strides[spatial_dim - 1], low_edge, high_edge)
    return values


def per_device(conserved, volume_fraction, cut_mask, merge_code):
    fields = conserved[0]
    fraction = volume_fraction[0]
    code_field = jnp.where(cut_mask[0] == 1, merge_code[0], 13)
    position = lax.axis_index("boxes")
    box_x = position // (NBY * NBZ)
    box_y = position // NBZ % NBY
    box_z = position % NBZ
    edges = (
        (box_x == 0, box_x == lax.axis_size("boxes") // (NBY * NBZ) - 1),
        (box_y == 0, box_y == NBY - 1),
        (box_z == 0, box_z == NBZ - 1),
    )
    members = decode(code_field)
    counts_ghost = count_members(members)[None]
    counts = sum_ghosts(counts_ghost, edges)[0]
    weight = fraction / counts
    packed = jnp.concatenate([weight[None], weight[None] * fields], axis=0)
    weighted = fill_ghosts(packed, 1, edges)
    average = neighbour_average(weighted, members)
    deposits = spread_back(average, members)
    gathered = sum_ghosts(deposits, edges)
    return (gathered / counts[None])[None]


def solution(mesh):
    return jax.shard_map(
        per_device,
        mesh=mesh,
        in_specs=(
            P("boxes", None, None, None, None),
            P("boxes", None, None, None),
            P("boxes", None, None, None),
            P("boxes", None, None, None),
        ),
        out_specs=P("boxes", None, None, None, None),
        check_vma=False,
    )
```

profile of v0, /device:TPU:129, one launch (start us, length us, event | category | flops | bytes accessed | tf_op | source)
XLA Modules:
  0.0 258.7 jit_solution(5698985412167638134)
XLA Ops:
  4.2 3.8 %add_bitcast_fusion = f32[1,18,34,130]{3,1,2,0:T(8,128)S(1)} fusion(f32[16,32,128]{2,0,1:T(8,128)S(1)} %broadcast_in_dim.486, pred[16,32,128]{2,0,1:T(8,128)(4,1)S(1)} %and.272, pred[16,32,128]{2,0,1:T(8,128)(4,1)S(1)} %get-tuple-element.36, pred[16,32,128]{2,0,1:T(8,128)(4,1)S(1)} %get-tuple-element.35, pred[16,32,128]{2,0,1:T(8,128)(4,1)S(1)} %get-tuple-element.113, ...), kind=kLoop, calls=%fused_computation.74 | loop fusion | flops 4137120 | bytes 2284320 | tf_op jit(solution)/shard_map/broadcast_in_dim | solution.py:127
  8.0 4.7 %collective-permute-start = (f32[1,1,34,130]{3,1,2,0:T(1,128)S(1)}, f32[1,1,34,130]{3,1,2,0:T(1,128)S(1)}, u32[]{:S(2)}, u32[]{:S(2)}) collective-permute-start(f32[1,1,34,130]{3,1,2,0:T(1,128)S(1)} %slice.283), channel_id=1, source_target_pairs={{0,16},{1,17},{2,18},{3,19},{4,20},{5,21},{6,22},{7,23},{8,24},{9,... | collective-permute-start | bytes 53048 | tf_op jit(solution)/shard_map/ppermute | solution.py:22
  12.7 3.6 %collective-permute-done = f32[1,1,34,130]{3,1,2,0:T(1,128)S(1)} collective-permute-done((f32[1,1,34,130]{3,1,2,0:T(1,128)S(1)}, f32[1,1,34,130]{3,1,2,0:T(1,128)S(1)}, u32[]{:S(2)}, u32[]{:S(2)}) %collective-permute-start) | collective-permute-done | bytes 17712 | tf_op jit(solution)/shard_map/ppermute | solution.py:22
  18.6 4.0 %collective-permute-done.1 = f32[1,1,34,130]{3,1,2,0:T(1,128)S(1)} collective-permute-done((f32[1,1,34,130]{3,1,2,0:T(1,128)S(1)}, f32[1,1,34,130]{3,1,2,0:T(1,128)S(1)}, u32[]{:S(2)}, u32[]{:S(2)}) %collective-permute-start.1) | collective-permute-done | bytes 17712 | tf_op jit(solution)/shard_map/ppermute | solution.py:22
  22.7 4.8 %collective-permute-start.2 = (f32[1,16,1,130]{3,1,2,0:T(8,128)S(1)}, f32[1,16,1,130]{3,1,2,0:T(8,128)S(1)}, u32[]{:S(2)}, u32[]{:S(2)}) collective-permute-start(f32[1,16,1,130]{3,1,2,0:T(8,128)S(1)} %pad_maximum_fusion.21), channel_id=1, source_target_pairs={{0,4},{1,5},{2,6},{3,7},{4,8},{5,9},{6,10},{7,11},{8,12},{9,13},{1... | collective-permute-start | bytes 24968 | tf_op jit(solution)/shard_map/ppermute | solution.py:22
  27.5 5.3 %collective-permute-done.2 = f32[1,16,1,130]{3,1,2,0:T(8,128)S(1)} collective-permute-done((f32[1,16,1,130]{3,1,2,0:T(8,128)S(1)}, f32[1,16,1,130]{3,1,2,0:T(8,128)S(1)}, u32[]{:S(2)}, u32[]{:S(2)}) %collective-permute-start.2) | collective-permute-done | bytes 8352 | tf_op jit(solution)/shard_map/ppermute | solution.py:22
  32.9 3.1 %collective-permute-start.3 = (f32[1,16,1,130]{3,1,2,0:T(8,128)S(1)}, f32[1,16,1,130]{3,1,2,0:T(8,128)S(1)}, u32[]{:S(2)}, u32[]{:S(2)}) collective-permute-start(f32[1,16,1,130]{3,1,2,0:T(8,128)S(1)} %get-tuple-element.83), channel_id=1, source_target_pairs={{4,0},{5,1},{6,2},{7,3},{8,4},{9,5},{10,6},{11,7},{12,8},{13,9},{1... | collective-permute-start | bytes 24968 | tf_op jit(solution)/shard_map/ppermute | solution.py:22
  39.1 8.4 %collective-permute-start.4 = (f32[1,16,32,1]{3,2,1,0:T(8,128)S(1)}, f32[1,16,32,1]{3,2,1,0:T(8,128)S(1)}, u32[]{:S(2)}, u32[]{:S(2)}) collective-permute-start(f32[1,16,32,1]{3,2,1,0:T(8,128)S(1)} %slice.289), channel_id=1, source_target_pairs={{0,1},{1,2},{2,3},{3,4},{4,5},{5,6},{6,7},{7,8},{8,9},{9,10},{10,1... | collective-permute-start | bytes 6152 | tf_op jit(solution)/shard_map/ppermute | solution.py:22
  47.5 3.3 %collective-permute-done.4 = f32[1,16,32,1]{3,2,1,0:T(8,128)S(1)} collective-permute-done((f32[1,16,32,1]{3,2,1,0:T(8,128)S(1)}, f32[1,16,32,1]{3,2,1,0:T(8,128)S(1)}, u32[]{:S(2)}, u32[]{:S(2)}) %collective-permute-start.4) | collective-permute-done | bytes 2080 | tf_op jit(solution)/shard_map/ppermute | solution.py:22
  51.0 8.6 %collective-permute-start.5 = (f32[1,16,32,1]{3,2,1,0:T(8,128)S(1)}, f32[1,16,32,1]{3,2,1,0:T(8,128)S(1)}, u32[]{:S(2)}, u32[]{:S(2)}) collective-permute-start(f32[1,16,32,1]{3,2,1,0:T(8,128)S(1)} %get-tuple-element.85), channel_id=1, source_target_pairs={{1,0},{2,1},{3,2},{4,3},{5,4},{6,5},{7,6},{8,7},{9,8},{10,9},{11,1... | collective-permute-start | bytes 6152 | tf_op jit(solution)/shard_map/ppermute | solution.py:22
  65.0 2.6 %copy.352 = f32[6,16,32,1]{2,1,3,0:T(8,128)} copy(f32[6,16,32,1]{3,2,1,0:T(8,128)} %get-tuple-element.51) | data formatting | bytes 24576
  71.9 4.2 %collective-permute-start.7 = (f32[6,16,32,1]{2,1,3,0:T(8,128)}, f32[6,16,32,1]{2,1,3,0:T(8,128)}, u32[]{:S(2)}, u32[]{:S(2)}) collective-permute-start(f32[6,16,32,1]{2,1,3,0:T(8,128)} %copy.353), channel_id=1, source_target_pairs={{1,0},{2,1},{3,2},{4,3},{5,4},{6,5},{7,6},{8,7},{9,8},{10,9},{11,1... | collective-permute-start | bytes 36872 | tf_op jit(solution)/shard_map/ppermute | solution.py:22
  76.1 2.6 %copy.332 = f32[6,16,32,1]{3,1,2,0:T(8,128)} copy(f32[6,16,32,1]{2,1,3,0:T(8,128)} %collective-permute-done.6) | data formatting | bytes 24576 | tf_op jit(solution)/shard_map/ppermute | solution.py:22
  80.3 2.7 %copy.334 = f32[6,16,32,1]{3,1,2,0:T(8,128)} copy(f32[6,16,32,1]{2,1,3,0:T(8,128)} %collective-permute-done.7) | data formatting | bytes 24576 | tf_op jit(solution)/shard_map/ppermute | solution.py:22
  88.0 9.3 %collective-permute-start.9 = (f32[6,16,1,130]{3,1,2,0:T(8,128)S(1)}, f32[6,16,1,130]{3,1,2,0:T(8,128)S(1)}, u32[]{:S(2)}, u32[]{:S(2)}) collective-permute-start(f32[6,16,1,130]{3,1,2,0:T(8,128)S(1)} %get-tuple-element.44), channel_id=1, source_target_pairs={{4,0},{5,1},{6,2},{7,3},{8,4},{9,5},{10,6},{11,7},{12,8},{13,9},{1... | collective-permute-start | bytes 149768 | tf_op jit(solution)/shard_map/ppermute | solution.py:22
  102.0 4.7 %maximum_maximum_fusion.1 = (f32[6,16,33,130]{3,1,2,0:T(8,128)}, f32[6,16,33,130]{3,1,2,0:T(8,128)}) fusion(f32[6,16,32,1]{3,1,2,0:T(8,128)S(1)} %broadcast_select_fusion, f32[6,16,32,128]{3,1,2,0:T(8,128)S(1)} %copy.336, f32[6,16,32,1]{3,1,2,0:T(8,128)S(1)} %broadcast_select_fusion.1, f32[6,16,1,130]{3,1,2,0:T(8,128)S(1)} %broadcast_select_fusion.35, ...), kind=kLoop, calls=%fused_computation.3 | loop fusion | flops 2471040 | bytes 4992000 | tf_op jit(solution)/shard_map/concatenate | solution.py:78
  106.7 7.0 %collective-permute-start.11 = (f32[6,1,34,130]{3,1,2,0:T(1,128)S(1)}, f32[6,1,34,130]{3,1,2,0:T(1,128)S(1)}, u32[]{:S(2)}, u32[]{:S(2)}) collective-permute-start(f32[6,1,34,130]{3,1,2,0:T(1,128)S(1)} %get-tuple-element.40), channel_id=1, source_target_pairs={{16,0},{17,1},{18,2},{19,3},{20,4},{21,5},{22,6},{23,7},{24,8},{25... | collective-permute-start | bytes 318248 | tf_op jit(solution)/shard_map/ppermute | solution.py:22
  116.7 6.3 %maximum_maximum_fusion = (f32[6,17,34,130]{3,1,2,0:T(8,128)S(1)}, f32[6,17,34,130]{3,1,2,0:T(8,128)S(1)}) fusion(f32[6,16,1,130]{3,1,2,0:T(8,128)S(1)} %broadcast_select_fusion.34, f32[6,16,32,1]{3,1,2,0:T(8,128)S(1)} %broadcast_select_fusion, f32[6,16,32,128]{3,1,2,0:T(8,128)} %copy-done, f32[6,16,32,1]{3,1,2,0:T(8,128)} %copy-done.1, ...), kind=kLoop, calls=%fused_computation | loop fusion | flops 4508400 | bytes 5516160 | tf_op jit(solution)/shard_map/concatenate | solution.py:78
  123.1 13.5 %fusion.2 = f32[6,16,32,128]{3,1,2,0:T(8,128)} fusion(f32[6,17,34,130]{3,1,2,0:T(8,128)S(1)} %get-tuple-element.38, f32[6,16,33,130]{3,1,2,0:T(8,128)} %get-tuple-element.42, f32[6,16,32,1]{3,1,2,0:T(8,128)} %copy-done.2, f32[6,16,32,128]{3,1,2,0:T(8,128)} %copy-done, f32[6,16,32,1]{3,1,2,0:T(8,128)} %copy-done.1, f32[6,16,33,130]{3,1,2,0:T(8,128)} %get-tuple-element.41, ...), kind=kLoop, calls=%fused_computation.15 | loop fusion | flops 21233664 | bytes 42622976 | tf_op jit(solution)/shard_map/add | solution.py:59
  139.4 2.9 %broadcast_select_fusion.25 = (f32[5,16,32,128]{3,1,2,0:T(8,128)S(1)}, f32[5,16,32,128]{3,1,2,0:T(8,128)S(1)}, f32[5,16,32,128]{3,1,2,0:T(8,128)}, f32[5,16,32,1...) fusion(f32[5,16,32,128]{3,1,2,0:T(8,128)S(1)} %get-tuple-element.6, ...), kind=kLoop, calls=%fused_computation.100 | loop fusion | flops 2293760 | bytes 10944512 | tf_op jit(solution)/shard_map/jit(_where)/select_n | solution.py:66
  142.4 4.1 %broadcast_select_fusion.26 = (f32[5,16,32,128]{3,1,2,0:T(8,128)S(1)}, f32[5,16,32,128]{3,1,2,0:T(8,128)S(1)}, f32[5,16,32,128]{3,1,2,0:T(8,128)S(1)}, f32[5,16,...) fusion(f32[5,16,32,128]{3,1,2,0:T(8,128)S(1)} %get-tuple-elemen, ...), kind=kLoop, calls=%fused_computation.101 | loop fusion | flops 5898240 | bytes 26083328 | tf_op jit(solution)/shard_map/jit(_where)/select_n | solution.py:66
  146.5 18.6 %pad_add_fusion = f32[5,18,34,130]{3,1,2,0:T(8,128)S(1)} fusion(f32[5,16,32,128]{3,1,2,0:T(8,128)} %get-tuple-element.77, f32[5,16,32,128]{3,1,2,0:T(8,128)S(1)} %get-tuple-element.54, f32[5,16,32,128]{3,1,2,0:T(8,128)S(1)} %get-tuple-element.55, f32[5,16,32,128]{3,1,2,0:T(8,128)S(1)} %get-tuple-element.56, f32[5,16,32,128]{3,1,2,0:T(8,128)S(1)} %get-tuple-element.57, ...), kind=kLoop, calls=%fused_computation.2 | loop fusion | flops 10342800 | bytes 36980640 | tf_op jit(solution)/shard_map/add | solution.py:66
  167.2 8.3 %collective-permute-done.12 = f32[5,1,34,130]{3,1,2,0:T(1,128)S(1)} collective-permute-done((f32[5,1,34,130]{3,1,2,0:T(1,128)S(1)}, f32[5,1,34,130]{3,1,2,0:T(1,128)S(1)}, u32[]{:S(2)}, u32[]{:S(2)}) %collective-permute-start.12) | collective-permute-done | bytes 88432 | tf_op jit(solution)/shard_map/ppermute | solution.py:22
  175.8 4.9 %collective-permute-start.13 = (f32[5,1,34,130]{3,1,2,0:T(1,128)S(1)}, f32[5,1,34,130]{3,1,2,0:T(1,128)S(1)}, u32[]{:S(2)}, u32[]{:S(2)}) collective-permute-start(f32[5,1,34,130]{3,1,2,0:T(1,128)S(1)} %get-tuple-element.46), channel_id=1, source_target_pairs={{16,0},{17,1},{18,2},{19,3},{20,4},{21,5},{22,6},{23,7},{24,8},{25... | collective-permute-start | bytes 265208 | tf_op jit(solution)/shard_map/ppermute | solution.py:22
  181.2 4.2 %collective-permute-done.13 = f32[5,1,34,130]{3,1,2,0:T(1,128)S(1)} collective-permute-done((f32[5,1,34,130]{3,1,2,0:T(1,128)S(1)}, f32[5,1,34,130]{3,1,2,0:T(1,128)S(1)}, u32[]{:S(2)}, u32[]{:S(2)}) %collective-permute-start.13) | collective-permute-done | bytes 88432 | tf_op jit(solution)/shard_map/ppermute | solution.py:22
  187.5 9.0 %collective-permute-done.14 = f32[5,16,1,130]{3,1,2,0:T(8,128)S(1)} collective-permute-done((f32[5,16,1,130]{3,1,2,0:T(8,128)S(1)}, f32[5,16,1,130]{3,1,2,0:T(8,128)S(1)}, u32[]{:S(2)}, u32[]{:S(2)}) %collective-permute-start.14) | collective-permute-done | bytes 41632 | tf_op jit(solution)/shard_map/ppermute | solution.py:22
  196.5 3.8 %collective-permute-start.15 = (f32[5,16,1,130]{3,1,2,0:T(8,128)S(1)}, f32[5,16,1,130]{3,1,2,0:T(8,128)S(1)}, u32[]{:S(2)}, u32[]{:S(2)}) collective-permute-start(f32[5,16,1,130]{3,1,2,0:T(8,128)S(1)} %get-tuple-element.48), channel_id=1, source_target_pairs={{4,0},{5,1},{6,2},{7,3},{8,4},{9,5},{10,6},{11,7},{12,8},{13,9},{1... | collective-permute-start | bytes 124808 | tf_op jit(solution)/shard_map/ppermute | solution.py:22
  208.6 11.2 %collective-permute-start.16 = (f32[5,16,32,1]{2,1,3,0:T(8,128)S(1)}, f32[5,16,32,1]{2,1,3,0:T(8,128)S(1)}, u32[]{:S(2)}, u32[]{:S(2)}) collective-permute-start(f32[5,16,32,1]{2,1,3,0:T(8,128)S(1)} %copy.339), channel_id=1, source_target_pairs={{0,1},{1,2},{2,3},{3,4},{4,5},{5,6},{6,7},{7,8},{8,9},{9,10},{10,1... | collective-permute-start | bytes 30728 | tf_op jit(solution)/shard_map/ppermute | solution.py:22
  219.7 5.7 %collective-permute-done.16 = f32[5,16,32,1]{2,1,3,0:T(8,128)S(1)} collective-permute-done((f32[5,16,32,1]{2,1,3,0:T(8,128)S(1)}, f32[5,16,32,1]{2,1,3,0:T(8,128)S(1)}, u32[]{:S(2)}, u32[]{:S(2)}) %collective-permute-start.16) | collective-permute-done | bytes 10272 | tf_op jit(solution)/shard_map/ppermute | solution.py:22
  227.0 3.3 %slice_add_fusion.1 = (f32[5,16,32,1]{3,1,2,0:T(8,128)}, f32[5,16,32,1]{3,1,2,0:T(8,128)}) fusion(f32[5,16,32,1]{3,1,2,0:T(8,128)} %copy.342, f32[5,16,32,130]{3,1,2,0:T(8,128)S(1)} %pad_maximum_fusion.4), kind=kLoop, calls=%fused_computation.70 | loop fusion | flops 2560 | bytes 51200 | tf_op jit(solution)/shard_map/add | solution.py:99
  232.2 10.0 %collective-permute-start.17 = (f32[5,16,32,1]{2,1,3,0:T(8,128)S(1)}, f32[5,16,32,1]{2,1,3,0:T(8,128)S(1)}, u32[]{:S(2)}, u32[]{:S(2)}) collective-permute-start(f32[5,16,32,1]{2,1,3,0:T(8,128)S(1)} %copy.344), channel_id=1, source_target_pairs={{1,0},{2,1},{3,2},{4,3},{5,4},{6,5},{7,6},{8,7},{9,8},{10,9},{11,1... | collective-permute-start | bytes 30728 | tf_op jit(solution)/shard_map/ppermute | solution.py:22
  255.5 3.1 %maximum_divide_fusion = f32[1,5,16,32,128]{4,3,2,1,0:T(8,128)} fusion(f32[1,5,16,32,1]{4,3,2,1,0:T(8,128)} %copy.351, f32[1,5,16,32,126]{4,3,2,1,0:T(8,128)S(1)} %copy-done.4, f32[1,5,16,32,1]{4,3,2,1,0:T(8,128)S(1)} %copy-done.5, f32[16,32,128]{2,1,0:T(8,128)S(1)} %copy-done.15), kind=kLoop, calls=%fused_computation.72 | loop fusion | flops 983040 | bytes 2883584 | tf_op jit(solution)/shard_map/div | solution.py:135
  (140 shorter events, 66.0 us)
Async XLA Ops:
  2.5 120.5 %copy-start.6 = (pred[1,16,32,128]{3,1,2,0:T(8,128)(4,1)}, pred[1,16,32,128]{3,1,2,0:T(8,128)(4,1)S(1)}, u32[]{:S(2)}) copy-start(pred[1,16,32,128]{3,1,2,0:T(8,128)(4,1)S(1)} %get-tuple-element.10) | copy-start | bytes 196612
  2.5 120.5 %copy-start.7 = (pred[1,16,32,128]{3,1,2,0:T(8,128)(4,1)}, pred[1,16,32,128]{3,1,2,0:T(8,128)(4,1)S(1)}, u32[]{:S(2)}) copy-start(pred[1,16,32,128]{3,1,2,0:T(8,128)(4,1)S(1)} %get-tuple-element.8) | copy-start | bytes 196612
  8.0 8.3 %collective-permute-start = (f32[1,1,34,130]{3,1,2,0:T(1,128)S(1)}, f32[1,1,34,130]{3,1,2,0:T(1,128)S(1)}, u32[]{:S(2)}, u32[]{:S(2)}) collective-permute-start(f32[1,1,34,130]{3,1,2,0:T(1,128)S(1)} %slice.283), channel_id=1, source_target_pairs={{0,16},{1,17},{2,18},{3,19},{4,20},{5,21},{6,22},{7,23},{8,24},{9,... | collective-permute-start | bytes 53048 | tf_op jit(solution)/shard_map/ppermute | solution.py:22
  16.4 6.2 %collective-permute-start.1 = (f32[1,1,34,130]{3,1,2,0:T(1,128)S(1)}, f32[1,1,34,130]{3,1,2,0:T(1,128)S(1)}, u32[]{:S(2)}, u32[]{:S(2)}) collective-permute-start(f32[1,1,34,130]{3,1,2,0:T(1,128)S(1)} %get-tuple-element.79), channel_id=1, source_target_pairs={{16,0},{17,1},{18,2},{19,3},{20,4},{21,5},{22,6},{23,7},{24,8},{25... | collective-permute-start | bytes 53048 | tf_op jit(solution)/shard_map/ppermute | solution.py:22
  22.7 10.2 %collective-permute-start.2 = (f32[1,16,1,130]{3,1,2,0:T(8,128)S(1)}, f32[1,16,1,130]{3,1,2,0:T(8,128)S(1)}, u32[]{:S(2)}, u32[]{:S(2)}) collective-permute-start(f32[1,16,1,130]{3,1,2,0:T(8,128)S(1)} %pad_maximum_fusion.21), channel_id=1, source_target_pairs={{0,4},{1,5},{2,6},{3,7},{4,8},{5,9},{6,10},{7,11},{8,12},{9,13},{1... | collective-permute-start | bytes 24968 | tf_op jit(solution)/shard_map/ppermute | solution.py:22
  32.9 6.0 %collective-permute-start.3 = (f32[1,16,1,130]{3,1,2,0:T(8,128)S(1)}, f32[1,16,1,130]{3,1,2,0:T(8,128)S(1)}, u32[]{:S(2)}, u32[]{:S(2)}) collective-permute-start(f32[1,16,1,130]{3,1,2,0:T(8,128)S(1)} %get-tuple-element.83), channel_id=1, source_target_pairs={{4,0},{5,1},{6,2},{7,3},{8,4},{9,5},{10,6},{11,7},{12,8},{13,9},{1... | collective-permute-start | bytes 24968 | tf_op jit(solution)/shard_map/ppermute | solution.py:22
  39.1 11.7 %collective-permute-start.4 = (f32[1,16,32,1]{3,2,1,0:T(8,128)S(1)}, f32[1,16,32,1]{3,2,1,0:T(8,128)S(1)}, u32[]{:S(2)}, u32[]{:S(2)}) collective-permute-start(f32[1,16,32,1]{3,2,1,0:T(8,128)S(1)} %slice.289), channel_id=1, source_target_pairs={{0,1},{1,2},{2,3},{3,4},{4,5},{5,6},{6,7},{7,8},{8,9},{9,10},{10,1... | collective-permute-start | bytes 6152 | tf_op jit(solution)/shard_map/ppermute | solution.py:22
  51.0 10.1 %collective-permute-start.5 = (f32[1,16,32,1]{3,2,1,0:T(8,128)S(1)}, f32[1,16,32,1]{3,2,1,0:T(8,128)S(1)}, u32[]{:S(2)}, u32[]{:S(2)}) collective-permute-start(f32[1,16,32,1]{3,2,1,0:T(8,128)S(1)} %get-tuple-element.85), channel_id=1, source_target_pairs={{1,0},{2,1},{3,2},{4,3},{5,4},{6,5},{7,6},{8,7},{9,8},{10,9},{11,1... | collective-permute-start | bytes 6152 | tf_op jit(solution)/shard_map/ppermute | solution.py:22
  60.8 25.8 %copy-start.11 = (pred[1,16,32,128]{3,1,2,0:T(8,128)(4,1)}, pred[1,16,32,128]{3,1,2,0:T(8,128)(4,1)S(1)}, u32[]{:S(2)}) copy-start(pred[1,16,32,128]{3,1,2,0:T(8,128)(4,1)S(1)} %get-tuple-element.87) | copy-start | bytes 196612
  60.8 62.2 %copy-start.10 = (pred[1,16,32,128]{3,1,2,0:T(8,128)(4,1)}, pred[1,16,32,128]{3,1,2,0:T(8,128)(4,1)S(1)}, u32[]{:S(2)}) copy-start(pred[1,16,32,128]{3,1,2,0:T(8,128)(4,1)S(1)} %get-tuple-element.20) | copy-start | bytes 196612
  67.7 8.5 %collective-permute-start.6 = (f32[6,16,32,1]{2,1,3,0:T(8,128)}, f32[6,16,32,1]{2,1,3,0:T(8,128)}, u32[]{:S(2)}, u32[]{:S(2)}) collective-permute-start(f32[6,16,32,1]{2,1,3,0:T(8,128)} %copy.352), channel_id=1, source_target_pairs={{0,1},{1,2},{2,3},{3,4},{4,5},{5,6},{6,7},{7,8},{8,9},{9,10},{10,1... | collective-permute-start | bytes 36872 | tf_op jit(solution)/shard_map/ppermute | solution.py:22
  70.7 31.3 %copy-start = (f32[6,16,32,128]{3,1,2,0:T(8,128)}, f32[6,16,32,128]{3,1,2,0:T(8,128)S(1)}, u32[]{:S(2)}) copy-start(f32[6,16,32,128]{3,1,2,0:T(8,128)S(1)} %copy.336) | copy-start | bytes 4718596
  71.9 8.4 %collective-permute-start.7 = (f32[6,16,32,1]{2,1,3,0:T(8,128)}, f32[6,16,32,1]{2,1,3,0:T(8,128)}, u32[]{:S(2)}, u32[]{:S(2)}) collective-permute-start(f32[6,16,32,1]{2,1,3,0:T(8,128)} %copy.353), channel_id=1, source_target_pairs={{1,0},{2,1},{3,2},{4,3},{5,4},{6,5},{7,6},{8,7},{9,8},{10,9},{11,1... | collective-permute-start | bytes 36872 | tf_op jit(solution)/shard_map/ppermute | solution.py:22
  80.3 21.7 %copy-start.1 = (f32[6,16,32,1]{3,1,2,0:T(8,128)}, f32[6,16,32,1]{3,1,2,0:T(8,128)S(1)}, u32[]{:S(2)}) copy-start(f32[6,16,32,1]{3,1,2,0:T(8,128)S(1)} %broadcast_select_fusion.1) | copy-start | bytes 36868
  84.6 32.0 %copy-start.2 = (f32[6,16,32,1]{3,1,2,0:T(8,128)}, f32[6,16,32,1]{3,1,2,0:T(8,128)S(1)}, u32[]{:S(2)}) copy-start(f32[6,16,32,1]{3,1,2,0:T(8,128)S(1)} %broadcast_select_fusion) | copy-start | bytes 36868
  84.7 12.5 %collective-permute-start.8 = (f32[6,16,1,130]{3,1,2,0:T(8,128)S(1)}, f32[6,16,1,130]{3,1,2,0:T(8,128)S(1)}, u32[]{:S(2)}, u32[]{:S(2)}) collective-permute-start(f32[6,16,1,130]{3,1,2,0:T(8,128)S(1)} %get-tuple-element.43), channel_id=1, source_target_pairs={{0,4},{1,5},{2,6},{3,7},{4,8},{5,9},{6,10},{7,11},{8,12},{9,13},{1... | collective-permute-start | bytes 149768 | tf_op jit(solution)/shard_map/ppermute | solution.py:22
  88.0 10.7 %collective-permute-start.9 = (f32[6,16,1,130]{3,1,2,0:T(8,128)S(1)}, f32[6,16,1,130]{3,1,2,0:T(8,128)S(1)}, u32[]{:S(2)}, u32[]{:S(2)}) collective-permute-start(f32[6,16,1,130]{3,1,2,0:T(8,128)S(1)} %get-tuple-element.44), channel_id=1, source_target_pairs={{4,0},{5,1},{6,2},{7,3},{8,4},{9,5},{10,6},{11,7},{12,8},{13,9},{1... | collective-permute-start | bytes 149768 | tf_op jit(solution)/shard_map/ppermute | solution.py:22
  100.0 13.6 %collective-permute-start.10 = (f32[6,1,34,130]{3,1,2,0:T(1,128)S(1)}, f32[6,1,34,130]{3,1,2,0:T(1,128)S(1)}, u32[]{:S(2)}, u32[]{:S(2)}) collective-permute-start(f32[6,1,34,130]{3,1,2,0:T(1,128)S(1)} %get-tuple-element.39), channel_id=1, source_target_pairs={{0,16},{1,17},{2,18},{3,19},{4,20},{5,21},{6,22},{7,23},{8,24},{9,... | collective-permute-start | bytes 318248 | tf_op jit(solution)/shard_map/ppermute | solution.py:22
  106.7 9.7 %collective-permute-start.11 = (f32[6,1,34,130]{3,1,2,0:T(1,128)S(1)}, f32[6,1,34,130]{3,1,2,0:T(1,128)S(1)}, u32[]{:S(2)}, u32[]{:S(2)}) collective-permute-start(f32[6,1,34,130]{3,1,2,0:T(1,128)S(1)} %get-tuple-element.40), channel_id=1, source_target_pairs={{16,0},{17,1},{18,2},{19,3},{20,4},{21,5},{22,6},{23,7},{24,8},{25... | collective-permute-start | bytes 318248 | tf_op jit(solution)/shard_map/ppermute | solution.py:22
  116.6 6.5 %copy-start.12 = (pred[1,16,32,128]{3,1,2,0:T(8,128)(4,1)S(1)}, pred[1,16,32,128]{3,1,2,0:T(8,128)(4,1)}, u32[]{:S(2)}) copy-start(pred[1,16,32,128]{3,1,2,0:T(8,128)(4,1)} %copy-done.11) | copy-start | bytes 196612
  116.6 6.5 %copy-start.14 = (pred[1,16,32,128]{3,1,2,0:T(8,128)(4,1)S(1)}, pred[1,16,32,128]{3,1,2,0:T(8,128)(4,1)}, u32[]{:S(2)}) copy-start(pred[1,16,32,128]{3,1,2,0:T(8,128)(4,1)} %get-tuple-element.95) | copy-start | bytes 196612
  116.6 6.5 %copy-start.16 = (pred[16,32,128]{2,0,1:T(8,128)(4,1)S(1)}, pred[16,32,128]{2,0,1:T(8,128)(4,1)}, u32[]{:S(2)}) copy-start(pred[16,32,128]{2,0,1:T(8,128)(4,1)} %get-tuple-element.7) | copy-start | bytes 196612
  116.6 6.5 %copy-start.17 = (pred[16,32,128]{2,0,1:T(8,128)(4,1)S(1)}, pred[16,32,128]{2,0,1:T(8,128)(4,1)}, u32[]{:S(2)}) copy-start(pred[16,32,128]{2,0,1:T(8,128)(4,1)} %get-tuple-element.97) | copy-start | bytes 196612
  116.6 6.5 %copy-start.18 = (pred[16,32,128]{2,0,1:T(8,128)(4,1)S(1)}, pred[16,32,128]{2,0,1:T(8,128)(4,1)}, u32[]{:S(2)}) copy-start(pred[16,32,128]{2,0,1:T(8,128)(4,1)} %get-tuple-element.98) | copy-start | bytes 196612
  116.6 6.5 %copy-start.19 = (pred[16,32,128]{2,0,1:T(8,128)(4,1)S(1)}, pred[16,32,128]{2,0,1:T(8,128)(4,1)}, u32[]{:S(2)}) copy-start(pred[16,32,128]{2,0,1:T(8,128)(4,1)} %get-tuple-element.100) | copy-start | bytes 196612
  116.6 6.5 %copy-start.20 = (pred[16,32,128]{2,0,1:T(8,128)(4,1)S(1)}, pred[16,32,128]{2,0,1:T(8,128)(4,1)}, u32[]{:S(2)}) copy-start(pred[16,32,128]{2,0,1:T(8,128)(4,1)} %get-tuple-element.101) | copy-start | bytes 196612
  165.3 10.2 %collective-permute-start.12 = (f32[5,1,34,130]{3,1,2,0:T(1,128)S(1)}, f32[5,1,34,130]{3,1,2,0:T(1,128)S(1)}, u32[]{:S(2)}, u32[]{:S(2)}) collective-permute-start(f32[5,1,34,130]{3,1,2,0:T(1,128)S(1)} %slice.324), channel_id=1, source_target_pairs={{0,16},{1,17},{2,18},{3,19},{4,20},{5,21},{6,22},{7,23},{8,24},{9,... | collective-permute-start | bytes 265208 | tf_op jit(solution)/shard_map/ppermute | solution.py:22
  175.8 9.5 %collective-permute-start.13 = (f32[5,1,34,130]{3,1,2,0:T(1,128)S(1)}, f32[5,1,34,130]{3,1,2,0:T(1,128)S(1)}, u32[]{:S(2)}, u32[]{:S(2)}) collective-permute-start(f32[5,1,34,130]{3,1,2,0:T(1,128)S(1)} %get-tuple-element.46), channel_id=1, source_target_pairs={{16,0},{17,1},{18,2},{19,3},{20,4},{21,5},{22,6},{23,7},{24,8},{25... | collective-permute-start | bytes 265208 | tf_op jit(solution)/shard_map/ppermute | solution.py:22
  185.6 10.9 %collective-permute-start.14 = (f32[5,16,1,130]{3,1,2,0:T(8,128)S(1)}, f32[5,16,1,130]{3,1,2,0:T(8,128)S(1)}, u32[]{:S(2)}, u32[]{:S(2)}) collective-permute-start(f32[5,16,1,130]{3,1,2,0:T(8,128)S(1)} %pad_maximum_fusion.19), channel_id=1, source_target_pairs={{0,4},{1,5},{2,6},{3,7},{4,8},{5,9},{6,10},{7,11},{8,12},{9,13},{1... | collective-permute-start | bytes 124808 | tf_op jit(solution)/shard_map/ppermute | solution.py:22
  196.5 6.7 %collective-permute-start.15 = (f32[5,16,1,130]{3,1,2,0:T(8,128)S(1)}, f32[5,16,1,130]{3,1,2,0:T(8,128)S(1)}, u32[]{:S(2)}, u32[]{:S(2)}) collective-permute-start(f32[5,16,1,130]{3,1,2,0:T(8,128)S(1)} %get-tuple-element.48), channel_id=1, source_target_pairs={{4,0},{5,1},{6,2},{7,3},{8,4},{9,5},{10,6},{11,7},{12,8},{13,9},{1... | collective-permute-start | bytes 124808 | tf_op jit(solution)/shard_map/ppermute | solution.py:22
  208.6 16.9 %collective-permute-start.16 = (f32[5,16,32,1]{2,1,3,0:T(8,128)S(1)}, f32[5,16,32,1]{2,1,3,0:T(8,128)S(1)}, u32[]{:S(2)}, u32[]{:S(2)}) collective-permute-start(f32[5,16,32,1]{2,1,3,0:T(8,128)S(1)} %copy.339), channel_id=1, source_target_pairs={{0,1},{1,2},{2,3},{3,4},{4,5},{5,6},{6,7},{7,8},{8,9},{9,10},{10,1... | collective-permute-start | bytes 30728 | tf_op jit(solution)/shard_map/ppermute | solution.py:22
  232.2 15.4 %collective-permute-start.17 = (f32[5,16,32,1]{2,1,3,0:T(8,128)S(1)}, f32[5,16,32,1]{2,1,3,0:T(8,128)S(1)}, u32[]{:S(2)}, u32[]{:S(2)}) collective-permute-start(f32[5,16,32,1]{2,1,3,0:T(8,128)S(1)} %copy.344), channel_id=1, source_target_pairs={{1,0},{2,1},{3,2},{4,3},{5,4},{6,5},{7,6},{8,7},{9,8},{10,9},{11,1... | collective-permute-start | bytes 30728 | tf_op jit(solution)/shard_map/ppermute | solution.py:22
  (16 other events, 46.2 us)
where the time goes:
time: 260 us; the launch traced here: 259 us
  starting transfers between devices  91.5 us (35%)
  other arithmetic  82.5 us (32%)
  waiting for transfers between devices  50.4 us (19%)
  local copies, waits for them, and re-layouts  33.3 us (13%)
    ppermute x18, starting transfers between devices, shifted(): return lax.ppermute(shard, axis, pairs)  91.5 us
    ppermute x18, waiting for transfers between devices, shifted(): return lax.ppermute(shard, axis, pairs)  50.4 us
    add x1, other arithmetic, spread_back(): running = running + placed(jnp.where(inside[None], average, 0.0), offset)  18.6 us
    add x1, other arithmetic, neighbour_average(): running + jnp.where(inside[None], window(weighted, offset, interior), 0.0)  13.5 us
    concatenate x2, other arithmetic, exchange_rims(): return jnp.concatenate([from_below, values, from_above], axis=spatial_dim)  11.1 us
    select_n x3, other arithmetic, spread_back(): running = running + placed(jnp.where(inside[None], average, 0.0), offset)  8.69 us
    unnamed x60, local copies, waits for them, and re-layouts  5.53 us
    ppermute x2, local copies, waits for them, and re-layouts, shifted(): return lax.ppermute(shard, axis, pairs)  5.32 us
  transfers between devices with their start and end apart: 18, of which 12 were waited for; matrix products, arithmetic and copies ran while one was open for 8% of the time, Pallas kernels for 0%

commit v1 on v0

v1 whole, which is shorter than its diff:
```python
import functools

import jax
import jax.numpy as jnp
from jax import lax
from jax.experimental import pallas as pl
from jax.experimental.pallas import tpu as pltpu
from jax.sharding import PartitionSpec as P

NBY = 4
NBZ = 4
CX, CY, CZ = 16, 32, 128
MESH = pl.DeviceIdType.MESH

ROWS = 48
SLOT = 40
SIGNS = [(dx, dy) for dx in (-1, 0, 1) for dy in (-1, 0, 1)]


def lanes_of(shape):
    return lax.broadcasted_iota(jnp.int32, shape, len(shape) - 1)


def roll_lanes(a, by):
    return pltpu.roll(a, by % CZ, a.ndim - 1) if by % CZ else a


def roll_rows(a, by):
    return pltpu.roll(a, by % a.shape[0], 0) if by % a.shape[0] else a


def decode(code):
    xy = jnp.floor((code + 0.5) * (1.0 / 3.0))
    x = jnp.floor((code + 0.5) * (1.0 / 9.0))
    return xy, xy - 3.0 * x, code - 3.0 * xy


def towards(xy, y, dx, dy):
    if dy == 0:
        return xy >= 6.0 if dx == 1 else xy <= 2.0
    if dx == 0:
        return y == 1.0 + dy
    return xy == 3.0 * (dx + 1) + (dy + 1)


def moved(a, dx, dy):
    return roll_rows(roll_lanes(a, 2 * dx), dy)


def plane_spread(a, xy, y):
    up = towards(xy, y, 1, 0)
    down = towards(xy, y, -1, 0)

    def along_x(b):
        return b + moved(jnp.where(up, b, 0.0), 1, 0) + moved(jnp.where(down, b, 0.0), -1, 0)

    total = along_x(a)
    for dy in (-1, 1):
        total = total + moved(along_x(jnp.where(towards(xy, y, 0, dy), a, 0.0)), 0, dy)
    return total


def plane_gather(a, xy, y):
    left, right = towards(xy, y, 0, -1), towards(xy, y, 0, 1)

    def along_y(b):
        return b + jnp.where(right, moved(b, 0, -1), jnp.where(left, moved(b, 0, 1), 0.0))

    ahead, behind = along_y(moved(a, -1, 0)), along_y(moved(a, 1, 0))
    chosen = jnp.where(towards(xy, y, 1, 0), ahead, jnp.where(towards(xy, y, -1, 0), behind, 0.0))
    return along_y(a) + chosen


def in_all_slots(a, lane):
    return jnp.where(lane < SLOT, a, jnp.where(lane < 2 * SLOT, roll_lanes(a, SLOT), roll_lanes(a, 2 * SLOT)))


def rim_planes(own, ghost, lane):
    lower = lane % 2 == 1

    def signs(code):
        xy, y, z = decode(code)
        return xy, y, jnp.where(lower, z, 2.0 - z)

    near_own, far_own = signs(own[2]), signs(roll_lanes(own[2], -SLOT))
    near_ghost, far_ghost = signs(ghost[2]), signs(roll_lanes(ghost[2], -SLOT))
    one = jnp.ones(own[0].shape, jnp.float32)

    def spread_ones(plane, sign):
        xy, y, z = plane
        return plane_spread(one if sign == 0 else jnp.where(z == 1.0 + sign, 1.0, 0.0), xy, y)

    entering = spread_ones(near_ghost, 1)
    ghost_count = spread_ones(near_ghost, 0) + spread_ones(far_ghost, 1) + spread_ones(near_own, -1)
    own_count = spread_ones(near_own, 0) + entering + spread_ones(far_own, -1)
    last = lane >= 2 * SLOT

    def weighted(pack, count):
        w = in_all_slots(roll_lanes(pack[1], -2 * SLOT) / count, lane)
        return w * pack[0], w * jnp.where(last, 1.0, pack[1])

    ghost_w = weighted(ghost, ghost_count)
    own_w = weighted(own, own_count)
    xy, y, z = signs(in_all_slots(ghost[2], lane))
    sums = [plane_gather(a + b, xy, y) for a, b in zip(ghost_w, own_w)]
    volume = in_all_slots(roll_lanes(sums[1], -2 * SLOT), lane)
    deposits = [plane_spread(jnp.where(z == 2.0, s / volume, 0.0), xy, y) for s in sums]
    return entering, ghost_w, deposits


def kernel(
    sizes, u_hbm, vf_hbm, mask_hbm, code_hbm, out_hbm,
    uv, code, xy_v, y_v, z_v, ones_v, mask_raw, code_raw, y_send, y_recv, rim_own, z_recv, rim_calc,
    w_v, up_v, down_v, inv_v, avg_v, out_v,
    load_sem, x_send_sem, x_recv_sem, y_send_sem, y_recv_sem, d_send_sem, d_recv_sem, z_send_sem, z_recv_sem, out_sem,
):
    nbx, nby, nbz = sizes
    me = lax.axis_index("boxes")
    bx, by, bz = me // (nby * nbz), (me // nbz) % nby, me % nbz
    has_x = (bx > 0, bx < nbx - 1)
    has_y = (by > 0, by < nby - 1)
    has_z = (bz > 0, bz < nbz - 1)
    steps = (-1, 1)

    loads = [
        pltpu.make_async_copy(mask_hbm, mask_raw, load_sem.at[0]),
        pltpu.make_async_copy(code_hbm, code_raw, load_sem.at[1]),
        pltpu.make_async_copy(vf_hbm, uv.at[0, 1:17, 8:40], load_sem.at[2]),
        pltpu.make_async_copy(u_hbm, uv.at[1:6, 1:17, 8:40], load_sem.at[3]),
    ]
    for load in loads:
        load.start()

    barrier = pltpu.get_barrier_semaphore()
    greeted = 0
    for i in (0, 1):
        for cond, target in (
            (has_x[i], me + steps[i] * nby * nbz), (has_y[i], me + steps[i] * nbz), (has_z[i], me + steps[i]),
        ):
            @pl.when(cond)
            def _(target=target):
                pl.semaphore_signal(barrier, inc=1, device_id=(target,), device_id_type=MESH)
            greeted = greeted + cond.astype(jnp.int32)
        for j in (0, 1):
            cond = has_x[i] & has_y[j]
            target = me + steps[i] * nby * nbz + steps[j] * nbz

            @pl.when(cond)
            def _(target=target):
                pl.semaphore_signal(barrier, inc=1, device_id=(target,), device_id_type=MESH)
            greeted = greeted + cond.astype(jnp.int32)

    loads[0].wait()
    loads[1].wait()

    def mask_code(x, _):
        code[x + 2, 8:40, :] = jnp.where(mask_raw[x] == 1, code_raw[x], 13).astype(jnp.float32)
        return _

    lax.fori_loop(0, CX, mask_code, 0)
    loads[2].wait()
    loads[3].wait()

    def pack_y(x, _):
        for s, near, far in ((0, 8, 9), (1, 39, 38)):
            for q in range(6):
                y_send[s, x, q:q + 1, :] = uv[q, x + 1, near:near + 1, :]
            y_send[s, x, 6:7, :] = code[x + 2, near:near + 1, :]
            y_send[s, x, 7:8, :] = code[x + 2, far:far + 1, :]
        return _

    lax.fori_loop(0, CX, pack_y, 0)
    pl.semaphore_wait(barrier, greeted)

    def x_copies(i):
        target = (me + steps[i] * nby * nbz,)
        src_u, dst_u = (1, 17) if i == 0 else (16, 0)
        src_c, dst_c = (2, 18) if i == 0 else (16, 0)
        return [
            pltpu.make_async_remote_copy(
                src_ref=uv.at[:, src_u, 8:40], dst_ref=uv.at[:, dst_u, 8:40], send_sem=x_send_sem.at[i, 0],
                recv_sem=x_recv_sem.at[1 - i, 0], device_id=target, device_id_type=MESH),
            pltpu.make_async_remote_copy(
                src_ref=code.at[pl.ds(src_c, 2), 8:40], dst_ref=code.at[pl.ds(dst_c, 2), 8:40],
                send_sem=x_send_sem.at[i, 1], recv_sem=x_recv_sem.at[1 - i, 1], device_id=target, device_id_type=MESH),
        ]

    def y_copy(i):
        return pltpu.make_async_remote_copy(
            src_ref=y_send.at[i], dst_ref=y_recv.at[1 - i, 2:18], send_sem=y_send_sem.at[i],
            recv_sem=y_recv_sem.at[1 - i], device_id=(me + steps[i] * nbz,), device_id_type=MESH)

    def d_copy(i, j):
        src, dst = (0, 18) if i == 0 else (14, 0)
        return pltpu.make_async_remote_copy(
            src_ref=y_send.at[j, pl.ds(src, 2)], dst_ref=y_recv.at[1 - j, pl.ds(dst, 2)], send_sem=d_send_sem.at[i, j],
            recv_sem=d_recv_sem.at[1 - i, 1 - j], device_id=(me + steps[i] * nby * nbz + steps[j] * nbz,),
            device_id_type=MESH)

    def z_copy(i):
        return pltpu.make_async_remote_copy(
            src_ref=rim_own, dst_ref=z_recv.at[1 - i], send_sem=z_send_sem.at[i], recv_sem=z_recv_sem.at[1 - i],
            device_id=(me + steps[i],), device_id_type=MESH)

    for i in (0, 1):
        @pl.when(has_x[i])
        def _(i=i):
            for copy in x_copies(i):
                copy.start()
    for j in (0, 1):
        @pl.when(has_y[j])
        def _(j=j):
            y_copy(j).start()
        for i in (0, 1):
            @pl.when(has_x[i] & has_y[j])
            def _(i=i, j=j):
                d_copy(i, j).start()

    for i in (0, 1):
        @pl.when(jnp.logical_not(has_x[i]))
        def _(i=i):
            u_at, c_at = (0, 0) if i == 0 else (17, 18)
            for q in range(6):
                uv[q, u_at, 8:40, :] = jnp.zeros((CY, CZ), jnp.float32)
            for c in (0, 1):
                code[c_at + c, 8:40, :] = jnp.full((CY, CZ), 13.0, jnp.float32)

        def blank(first, count, j):
            row = lax.broadcasted_iota(jnp.int32, (8, CZ), 0)
            for x in range(count):
                y_recv[j, first + x] = jnp.where(row < 6, 0.0, 13.0)

        @pl.when(jnp.logical_not(has_y[i]))
        def _(i=i):
            blank(2, CX, i)

        for j in (0, 1):
            @pl.when(jnp.logical_not(has_x[i] & has_y[j]))
            def _(i=i, j=j):
                blank(0 if i == 0 else 18, 2, j)

    for s in (0, 1):
        @pl.when(has_y[s])
        def _(s=s):
            y_copy(1 - s).wait_recv()
        for i in (0, 1):
            @pl.when(has_x[i] & has_y[s])
            def _(i=i, s=s):
                d_copy(1 - i, 1 - s).wait_recv()
        @pl.when(has_x[s])
        def _(s=s):
            for copy in x_copies(1 - s):
                copy.wait_recv()

    def unpack_y(x, _):
        for s, near, far in ((0, 7, 6), (1, 40, 41)):
            code[x, near:near + 1, :] = y_recv[s, x, 6:7, :]
            code[x, far:far + 1, :] = y_recv[s, x, 7:8, :]
        return _

    def unpack_u(x, _):
        for s, near in ((0, 7), (1, 40)):
            for q in range(6):
                uv[q, x, near:near + 1, :] = y_recv[s, x + 1, q:q + 1, :]
        return _

    lax.fori_loop(0, 20, unpack_y, 0)
    lax.fori_loop(0, 18, unpack_u, 0)

    lane8 = lanes_of((8, CZ))

    def pack_rims(t, _):
        base = 6 + 8 * t
        blocks = [jnp.zeros((8, CZ), jnp.float32) for _ in range(3)]

        def place(block, value, slot, x):
            shift = slot * SLOT + 2 * x + 1
            hit = (lane8 // 2) == (slot * SLOT + 2 * x) // 2
            return jnp.where(hit, roll_lanes(value, shift), block)

        for x in range(20):
            near = code[x, pl.ds(base, 8), :]
            far = jnp.where(lane8 == CZ - 1, roll_lanes(near, 1), roll_lanes(near, -1))
            blocks[2] = place(blocks[2], near, 0, x)
            blocks[2] = place(blocks[2], far, 1, x)
            if 1 <= x <= 18:
                for q in range(5):
                    blocks[q // 3] = place(blocks[q // 3], uv[q + 1, x - 1, pl.ds(base, 8), :], q % 3, x)
                blocks[1] = place(blocks[1], uv[0, x - 1, pl.ds(base, 8), :], 2, x)
        for b in range(3):
            rim_own[b, pl.ds(pl.multiple_of(8 * t, 8), 8), :] = blocks[b]
        return _

    lax.fori_loop(0, 5, pack_rims, 0)
    for i in (0, 1):
        @pl.when(has_z[i])
        def _(i=i):
            z_copy(i).start()

        @pl.when(jnp.logical_not(has_z[i]))
        def _(i=i):
            for b in range(3):
                z_recv[i, b] = jnp.full((40, CZ), 13.0 if b == 2 else 0.0, jnp.float32)

    def signs(x, _):
        for t in range(5):
            rows = slice(6 + 8 * t, 14 + 8 * t)
            xy, y, z = decode(code[x, rows, :])
            xy_v[x, rows, :] = xy
            y_v[x, rows, :] = y
            z_v[x, rows, :] = z
            ones_v[x, rows, :] = jnp.where(z == 2.0, 257, jnp.where(z == 0.0, 65537, 1))
        return _

    lax.fori_loop(0, 20, signs, 0)

    for i in (0, 1):
        @pl.when(has_z[i])
        def _(i=i):
            z_copy(1 - i).wait_recv()

    lane40 = lanes_of((40, CZ))
    own = [rim_own[b] for b in range(3)]
    ghost = [jnp.where(lane40 % 2 == 1, roll_lanes(z_recv[0, b], 1), roll_lanes(z_recv[1, b], -1)) for b in range(3)]
    entering, ghost_w, deposits = rim_planes(own, ghost, lane40)
    for k, a in enumerate((entering, *ghost_w, *deposits)):
        rim_calc[k, 0:40, :] = a

    first, final = lane8 == 0, lane8 == CZ - 1

    def at_edges(k, slot, x, row):
        shift = CZ * 2 - (slot * SLOT + 2 * x + 1)
        return pltpu.roll(rim_calc[k, row:row + 8, :], lax.rem(shift, CZ), 1)

    def weights(x, _):
        for t in range(5):
            top = 7 + 8 * t
            rows = slice(top, top + 8)
            total = ones_v[x + 1, rows, :]
            for dx, dy in SIGNS:
                if (dx, dy) != (0, 0):
                    at = slice(top - dy, top - dy + 8)
                    hit = towards(xy_v[x + 1 - dx, at, :], y_v[x + 1 - dx, at, :], dx, dy)
                    total = total + jnp.where(hit, ones_v[x + 1 - dx, at, :], 0)
            here = (total & 255).astype(jnp.float32)
            up = ((total >> 8) & 255).astype(jnp.float32)
            down = (total >> 16).astype(jnp.float32)
            edge = at_edges(0, 0, x + 1, top - 6)
            count = here + jnp.where(first, edge, roll_lanes(up, 1)) + jnp.where(final, edge, roll_lanes(down, -1))
            inv = 1.0 / count
            inv_v[x, rows, :] = inv
            w = uv[0, x, rows, :] * inv
            for q in range(6):
                value = w if q == 0 else w * uv[q, x, rows, :]
                k, slot = (2, 2) if q == 0 else (1 + (q - 1) // 3, (q - 1) % 3)
                edge = at_edges(k, slot, x + 1, top - 6)
                w_v[q, x + 1, rows, :] = value
                up_v[q, x + 1, rows, :] = value + jnp.where(final, edge, roll_lanes(value, -1))
                down_v[q, x + 1, rows, :] = value + jnp.where(first, edge, roll_lanes(value, 1))
        return _

    lax.fori_loop(0, 18, weights, 0)

    def gather(x, _):
        for t in range(5):
            top = 7 + 8 * t
            rows = slice(top, top + 8)
            xy, y, z = xy_v[x + 1, rows, :], y_v[x + 1, rows, :], z_v[x + 1, rows, :]
            x_up, x_down = towards(xy, y, 1, 0), towards(xy, y, -1, 0)
            y_up, y_down = y == 2.0, y == 0.0
            z_up, z_down = z == 2.0, z == 0.0

            def total(q):
                def line(dx, dy):
                    at = slice(top + dy, top + dy + 8)
                    return jnp.where(z_up, up_v[q, x + 1 + dx, at, :], jnp.where(
                        z_down, down_v[q, x + 1 + dx, at, :], w_v[q, x + 1 + dx, at, :]))

                def plane(dx):
                    return line(dx, 0) + jnp.where(y_up, line(dx, 1), jnp.where(y_down, line(dx, -1), 0.0))

                return plane(0) + jnp.where(x_up, plane(1), jnp.where(x_down, plane(-1), 0.0))

            inv = 1.0 / total(0)
            for q in range(5):
                avg_v[q, x, rows, :] = total(q + 1) * inv
        return _

    lax.fori_loop(0, 18, gather, 0)

    def scatter(x, _):
        for t in range(4):
            top = 8 + 8 * t
            rows = slice(top, top + 8)
            here = [None] * 5
            up = [None] * 5
            down = [None] * 5
            for dx, dy in SIGNS:
                at = slice(top - dy, top - dy + 8)
                z = z_v[x + 2 - dx, at, :]
                z_up, z_down = z == 2.0, z == 0.0
                hit = None
                if (dx, dy) != (0, 0):
                    hit = towards(xy_v[x + 2 - dx, at, :], y_v[x + 2 - dx, at, :], dx, dy)
                    z_up, z_down = hit & z_up, hit & z_down
                for q in range(5):
                    a = avg_v[q, x + 1 - dx, at, :]
                    terms = (a if hit is None else jnp.where(hit, a, 0.0), jnp.where(z_up, a, 0.0), jnp.where(z_down, a, 0.0))
                    here[q], up[q], down[q] = (
                        new if old is None else old + new for old, new in zip((here[q], up[q], down[q]), terms))
            inv = inv_v[x + 1, rows, :]
            for q in range(5):
                edge = at_edges(3 + q // 3, q % 3, x + 2, top - 6)
                total = here[q] + jnp.where(first, edge, roll_lanes(up[q], 1)) + jnp.where(
                    final, edge, roll_lanes(down[q], -1))
                out_v[q, x, 8 * t:8 * t + 8, :] = total * inv
        return _

    lax.fori_loop(0, CX, scatter, 0)
    out_copy = pltpu.make_async_copy(out_v, out_hbm, out_sem)
    out_copy.start()

    for i in (0, 1):
        @pl.when(has_x[i])
        def _(i=i):
            for copy in x_copies(i):
                copy.wait_send()

        @pl.when(has_y[i])
        def _(i=i):
            y_copy(i).wait_send()

        for j in (0, 1):
            @pl.when(has_x[i] & has_y[j])
            def _(i=i, j=j):
                d_copy(i, j).wait_send()

        @pl.when(has_z[i])
        def _(i=i):
            z_copy(i).wait_send()
    out_copy.wait()


def solution(mesh, nby=NBY, nbz=NBZ):
    nbx = mesh.shape["boxes"] // (nby * nbz)
    f32 = jnp.float32

    def per_device(conserved, volume_fraction, cut_mask, merge_code):
        dma = pltpu.SemaphoreType.DMA
        out = pl.pallas_call(
            functools.partial(kernel, (nbx, nby, nbz)),
            out_shape=jax.ShapeDtypeStruct((5, CX, CY, CZ), f32),
            in_specs=[pl.BlockSpec(memory_space=pl.ANY)] * 4,
            out_specs=pl.BlockSpec(memory_space=pl.ANY),
            scratch_shapes=[
                pltpu.VMEM((6, 18, ROWS, CZ), f32),
                pltpu.VMEM((20, ROWS, CZ), f32),
                pltpu.VMEM((20, ROWS, CZ), f32),
                pltpu.VMEM((20, ROWS, CZ), f32),
                pltpu.VMEM((20, ROWS, CZ), f32),
                pltpu.VMEM((20, ROWS, CZ), jnp.int32),
                pltpu.VMEM((CX, CY, CZ), jnp.int32),
                pltpu.VMEM((CX, CY, CZ), jnp.int32),
                pltpu.VMEM((2, CX, 8, CZ), f32),
                pltpu.VMEM((2, 20, 8, CZ), f32),
                pltpu.VMEM((3, 40, CZ), f32),
                pltpu.VMEM((2, 3, 40, CZ), f32),
                pltpu.VMEM((5, ROWS, CZ), f32),
                pltpu.VMEM((6, 20, ROWS, CZ), f32),
                pltpu.VMEM((6, 20, ROWS, CZ), f32),
                pltpu.VMEM((6, 20, ROWS, CZ), f32),
                pltpu.VMEM((18, ROWS, CZ), f32),
                pltpu.VMEM((5, 18, ROWS, CZ), f32),
                pltpu.VMEM((5, CX, CY, CZ), f32),
                dma((4,)), dma((2, 2)), dma((2, 2)), dma((2,)), dma((2,)), dma((2, 2)), dma((2, 2)), dma((2,)), dma((2,)),
                dma,
            ],
            compiler_params=pltpu.CompilerParams(
                collective_id=0, has_side_effects=True, vmem_limit_bytes=60 * 1024 * 1024
            ),
        )(conserved[0], volume_fraction[0], cut_mask[0], merge_code[0])
        return out[None]

    return jax.shard_map(
        per_device,
        mesh=mesh,
        in_specs=(
            P("boxes", None, None, None, None),
            P("boxes", None, None, None),
            P("boxes", None, None, None),
            P("boxes", None, None, None),
        ),
        out_specs=P("boxes", None, None, None, None),
        check_vma=False,
    )
```

time: 260 us -> 38.9 us (0.15)
  the two profiles are of different devices: /device:TPU:129 before, /device:TPU:51 now
where the time goes in v1:
time: 38.9 us; the launch traced here: 38.8 us
  Pallas kernels  36.3 us (93%)
  local copies, waits for them, and re-layouts  2.52 us (6%)
    pallas_call x1, Pallas kernels, per_device(): pl.pallas_call(functools.partial(kernel, (nbx, nby, nbz)), out_shape=jax....  36.3 us
    unnamed x1, local copies, waits for them, and re-layouts  2.52 us

profile of v1, /device:TPU:51, one launch (start us, length us, event | category | flops | bytes accessed | tf_op | source)
XLA Modules:
  0.0 38.8 jit_solution(14216882611549562588)
XLA Ops:
  0.0 36.3 %shard_map.46 = f32[5,16,32,128]{3,2,1,0:T(8,128)} custom-call(f32[5,16,32,128]{3,2,1,0:T(8,128)} %bitcast.6, f32[16,32,128]{2,1,0:T(8,128)} %bitcast.7, s32[16,32,128]{2,1,0:T(8,128)} %bitcast.8, s32[16,32,128]{2,1,0:T(8,128)} %bitcast.9), custom_call_target="tpu_custom_call" | custom-call | tf_op jit(solution)/shard_map/pallas_call | solution.py:450
  36.3 2.5 %copy.6 = f32[1,5,16,32,128]{4,3,2,1,0:T(8,128)} copy(f32[1,5,16,32,128]{4,3,2,1,0:T(8,128)} %bitcast.5) | data formatting | bytes 2621440

commit v2 on v0

v2 whole, which is shorter than its diff:
```python
import functools

import jax
import jax.numpy as jnp
from jax import lax
from jax.experimental import pallas as pl
from jax.experimental.pallas import tpu as pltpu
from jax.sharding import PartitionSpec as P

NBY = 4
NBZ = 4
CX, CY, CZ = 16, 32, 128
MESH = pl.DeviceIdType.MESH

ROWS = 48
SLOT = 40
SIGNS = [(dx, dy) for dx in (-1, 0, 1) for dy in (-1, 0, 1)]


def lanes_of(shape):
    return lax.broadcasted_iota(jnp.int32, shape, len(shape) - 1)


def roll_lanes(a, by):
    return pltpu.roll(a, by % CZ, a.ndim - 1) if by % CZ else a


def roll_rows(a, by):
    return pltpu.roll(a, by % a.shape[0], 0) if by % a.shape[0] else a


def decode(code):
    xy = jnp.floor((code + 0.5) * (1.0 / 3.0))
    x = jnp.floor((code + 0.5) * (1.0 / 9.0))
    return xy, xy - 3.0 * x, code - 3.0 * xy


def towards(xy, y, dx, dy):
    if dy == 0:
        return xy >= 6.0 if dx == 1 else xy <= 2.0
    if dx == 0:
        return y == 1.0 + dy
    return xy == 3.0 * (dx + 1) + (dy + 1)


def moved(a, dx, dy):
    return roll_rows(roll_lanes(a, 2 * dx), dy)


def plane_spread(a, xy, y):
    up = towards(xy, y, 1, 0)
    down = towards(xy, y, -1, 0)

    def along_x(b):
        return b + moved(jnp.where(up, b, 0.0), 1, 0) + moved(jnp.where(down, b, 0.0), -1, 0)

    total = along_x(a)
    for dy in (-1, 1):
        total = total + moved(along_x(jnp.where(towards(xy, y, 0, dy), a, 0.0)), 0, dy)
    return total


def plane_gather(a, xy, y):
    left, right = towards(xy, y, 0, -1), towards(xy, y, 0, 1)

    def along_y(b):
        return b + jnp.where(right, moved(b, 0, -1), jnp.where(left, moved(b, 0, 1), 0.0))

    ahead, behind = along_y(moved(a, -1, 0)), along_y(moved(a, 1, 0))
    chosen = jnp.where(towards(xy, y, 1, 0), ahead, jnp.where(towards(xy, y, -1, 0), behind, 0.0))
    return along_y(a) + chosen


def in_all_slots(a, lane):
    return jnp.where(lane < SLOT, a, jnp.where(lane < 2 * SLOT, roll_lanes(a, SLOT), roll_lanes(a, 2 * SLOT)))


def rim_planes(own, ghost, lane):
    lower = lane % 2 == 1

    def signs(code):
        xy, y, z = decode(code)
        return xy, y, jnp.where(lower, z, 2.0 - z)

    near_own, far_own = signs(own[2]), signs(roll_lanes(own[2], -SLOT))
    near_ghost, far_ghost = signs(ghost[2]), signs(roll_lanes(ghost[2], -SLOT))
    one = jnp.ones(own[0].shape, jnp.float32)

    def spread_ones(plane, sign):
        xy, y, z = plane
        return plane_spread(one if sign == 0 else jnp.where(z == 1.0 + sign, 1.0, 0.0), xy, y)

    entering = spread_ones(near_ghost, 1)
    ghost_count = spread_ones(near_ghost, 0) + spread_ones(far_ghost, 1) + spread_ones(near_own, -1)
    own_count = spread_ones(near_own, 0) + entering + spread_ones(far_own, -1)
    last = lane >= 2 * SLOT

    def weighted(pack, count):
        w = in_all_slots(roll_lanes(pack[1], -2 * SLOT) / count, lane)
        return w * pack[0], w * jnp.where(last, 1.0, pack[1])

    ghost_w = weighted(ghost, ghost_count)
    own_w = weighted(own, own_count)
    xy, y, z = signs(in_all_slots(ghost[2], lane))
    sums = [plane_gather(a + b, xy, y) for a, b in zip(ghost_w, own_w)]
    volume = in_all_slots(roll_lanes(sums[1], -2 * SLOT), lane)
    deposits = [plane_spread(jnp.where(z == 2.0, s / volume, 0.0), xy, y) for s in sums]
    return entering, ghost_w, deposits


TILES = 5


def kernel(
    sizes, u_hbm, vf_hbm, mask_hbm, code_hbm, out_ref,
    uv, code, xy_v, y_v, z_v, xz_v, yz_v, ones_v, total_v, mask_raw, code_raw, y_send, y_recv, rim_own, rim_ghost, rim_x,
    rim_ghost_x, rim_calc, w_v, up_v, down_v, inv_v, avg_v,
    load_sem, x_send_sem, x_recv_sem, y_send_sem, y_recv_sem, d_send_sem, d_recv_sem, z_send_sem, z_recv_sem,
    yz_send_sem, yz_recv_sem, zx_send_sem, zx_recv_sem,
):
    nbx, nby, nbz = sizes
    me = lax.axis_index("boxes")
    bx, by, bz = me // (nby * nbz), (me // nbz) % nby, me % nbz
    has_x = (bx > 0, bx < nbx - 1)
    has_y = (by > 0, by < nby - 1)
    has_z = (bz > 0, bz < nbz - 1)
    has_yz = [[has_y[j] & has_z[i] for i in (0, 1)] for j in (0, 1)]
    steps = (-1, 1)
    x_step, y_step = nby * nbz, nbz

    def when(cond):
        return pl.when(cond)

    barrier = pltpu.get_barrier_semaphore()
    greeted = 0
    for i in (0, 1):
        met = [(has_x[i], steps[i] * x_step), (has_y[i], steps[i] * y_step), (has_z[i], steps[i])]
        met += [(has_yz[j][i], steps[j] * y_step + steps[i]) for j in (0, 1)]
        for cond, step in met:
            @when(cond)
            def _(step=step):
                pl.semaphore_signal(barrier, inc=1, device_id=(me + step,), device_id_type=MESH)
            greeted = greeted + cond.astype(jnp.int32)

    loads = [
        pltpu.make_async_copy(mask_hbm, mask_raw, load_sem.at[0]),
        pltpu.make_async_copy(code_hbm, code_raw, load_sem.at[1]),
        pltpu.make_async_copy(vf_hbm, uv.at[0, 2:18, 8:40], load_sem.at[2]),
        pltpu.make_async_copy(u_hbm, uv.at[1:6, 2:18, 8:40], load_sem.at[3]),
    ]
    for load in loads:
        load.start()

    def remote(src, dst, send, recv, step):
        return pltpu.make_async_remote_copy(
            src_ref=src, dst_ref=dst, send_sem=send, recv_sem=recv, device_id=(me + step,), device_id_type=MESH)

    def x_copies(i):
        src_u, dst_u = (2, 18) if i == 0 else (17, 1)
        src_c, dst_c = (2, 18) if i == 0 else (16, 0)
        return [
            remote(uv.at[:, src_u, 8:40], uv.at[:, dst_u, 8:40], x_send_sem.at[i, 0], x_recv_sem.at[1 - i, 0],
                   steps[i] * x_step),
            remote(code.at[pl.ds(src_c, 2), 8:40], code.at[pl.ds(dst_c, 2), 8:40], x_send_sem.at[i, 1],
                   x_recv_sem.at[1 - i, 1], steps[i] * x_step),
        ]

    def d_copy(i):
        src, dst = (2, 18) if i == 0 else (16, 0)
        return remote(y_recv.at[:, pl.ds(src, 2)], y_recv.at[:, pl.ds(dst, 2)], d_send_sem.at[i], d_recv_sem.at[1 - i],
                      steps[i] * x_step)

    rim_src, rim_dst = (8, 32), (40, 0)

    def y_copies(i, which=None):
        return [
            remote(y_send.at[i], y_recv.at[1 - i, 2:18], y_send_sem.at[i, 0], y_recv_sem.at[1 - i, 0], steps[i] * y_step),
        ] * (which != 1) + [
            remote(rim_own.at[:, pl.ds(rim_src[i], 8)], rim_own.at[:, pl.ds(rim_dst[i], 8)], y_send_sem.at[i, 1],
                   y_recv_sem.at[1 - i, 1], steps[i] * y_step),
        ] * (which != 0)

    def z_copy(i):
        return remote(rim_own.at[:, 8:40], rim_ghost.at[1 - i, :, 8:40], z_send_sem.at[i], z_recv_sem.at[1 - i], steps[i])

    def yz_copy(j, i):
        return remote(
            rim_own.at[:, pl.ds(rim_src[j], 8)], rim_ghost.at[1 - i, :, pl.ds(rim_dst[j], 8)], yz_send_sem.at[j, i],
            yz_recv_sem.at[1 - j, 1 - i], steps[j] * y_step + steps[i])

    def zx_copy(i):
        return remote(rim_x, rim_ghost_x.at[1 - i], zx_send_sem.at[i], zx_recv_sem.at[1 - i], steps[i])

    loads[0].wait()
    loads[1].wait()

    def write_signs(X, base):
        rows = pl.ds(base, 8)
        c = code[X, rows, :]
        xy, y, z = decode(c)
        xy_v[X, rows, :] = xy
        y_v[X, rows, :] = y
        z_v[X, rows, :] = z
        xz_v[X, rows, :] = xy - y + z
        yz_v[X, rows, :] = 3.0 * y + z
        ones_v[X, rows, :] = jnp.where(z == 2.0, 257, jnp.where(z == 0.0, 65537, 1))

    def own_codes(x, _):
        code[x + 2, 8:40, :] = jnp.where(mask_raw[x] == 1, code_raw[x], 13).astype(jnp.float32)
        return _

    lax.fori_loop(0, CX, own_codes, 0)
    loads[2].wait()
    loads[3].wait()

    def pack_y(x, _):
        for s, near, far in ((0, 8, 9), (1, 39, 38)):
            for q in range(6):
                y_send[s, x, q:q + 1, :] = uv[q, x + 2, near:near + 1, :]
            y_send[s, x, 6:7, :] = code[x + 2, near:near + 1, :]
            y_send[s, x, 7:8, :] = code[x + 2, far:far + 1, :]
        return _

    lax.fori_loop(0, CX, pack_y, 0)
    lane8 = lanes_of((8, CZ))

    def pack_rims(rim, slabs, base):
        blocks = [jnp.zeros((8, CZ), jnp.float32) for _ in range(3)]

        def place(b, value, slot, X):
            lane = slot * SLOT + 2 * X
            blocks[b] = jnp.where(lane8 // 2 == lane // 2, roll_lanes(value, lane + 1), blocks[b])

        for X in slabs:
            near = code[X, pl.ds(base, 8), :]
            place(2, near, 0, X)
            place(2, jnp.where(lane8 == CZ - 1, roll_lanes(near, 1), roll_lanes(near, -1)), 1, X)
            if 1 <= X <= 18:
                for q in range(5):
                    place(q // 3, uv[q + 1, X, pl.ds(base, 8), :], q % 3, X)
                place(1, uv[0, X, pl.ds(base, 8), :], 2, X)
        for b in range(3):
            rim[b, pl.ds(base, 8), :] = blocks[b]

    def pack_own_rims(t, _):
        pack_rims(rim_own, range(2, 18), pl.multiple_of(8 + 8 * t, 8))
        return _

    lax.fori_loop(0, 4, pack_own_rims, 0)
    pl.semaphore_wait(barrier, greeted)

    for i in (0, 1):
        @when(has_y[i])
        def _(i=i):
            for copy in y_copies(i):
                copy.start()

        @when(has_z[i])
        def _(i=i):
            z_copy(i).start()

        for j in (0, 1):
            @when(has_yz[j][i])
            def _(i=i, j=j):
                yz_copy(j, i).start()
    for i in (0, 1):
        @when(has_x[i])
        def _(i=i):
            for copy in x_copies(i):
                copy.start()

    tile_row = lax.broadcasted_iota(jnp.int32, (8, CZ), 0)

    def blank_rim(rim, first, rows):
        for b in range(3):
            rim[b, first:first + rows, :] = jnp.full((rows, CZ), 13.0 if b == 2 else 0.0, jnp.float32)

    for s in (0, 1):
        @when(jnp.logical_not(has_y[s]))
        def _(s=s):
            blank_rim(rim_own, 0 if s == 0 else 40, 8)
            for X in range(2, 18):
                y_recv[s, X] = jnp.where(tile_row < 6, 0.0, 13.0)

        @when(jnp.logical_not(has_z[s]))
        def _(s=s):
            blank_rim(rim_ghost.at[s], 8, 32)
            blank_rim(rim_ghost_x.at[s], 0, ROWS)

        for j in (0, 1):
            @when(jnp.logical_not(has_yz[j][s]))
            def _(s=s, j=j):
                blank_rim(rim_ghost.at[s], 0 if j == 0 else 40, 8)

        @when(jnp.logical_not(has_x[s]))
        def _(s=s):
            u_at, c_at = (1, 0) if s == 0 else (18, 18)
            for q in range(6):
                uv[q, u_at, 8:40, :] = jnp.zeros((CY, CZ), jnp.float32)
            for c in (0, 1):
                code[c_at + c, 8:40, :] = jnp.full((CY, CZ), 13.0, jnp.float32)
                for j in (0, 1):
                    y_recv[j, c_at + c] = jnp.where(tile_row < 6, 0.0, 13.0)

    def count(X, tiles):
        for t in tiles:
            top = 7 + 8 * t
            total = ones_v[X, top:top + 8, :]
            for dx, dy in SIGNS:
                if (dx, dy) != (0, 0):
                    at = slice(top - dy, top - dy + 8)
                    signs = (y_v if dx == 0 else xy_v)[X - dx, at, :]
                    total = total + jnp.where(towards(signs, signs, dx, dy), ones_v[X - dx, at, :], 0)
            total_v[X, top:top + 8, :] = total

    first, final = lane8 == 0, lane8 == CZ - 1

    def at_edges(k, slot, X, top):
        shift = CZ * 2 - (slot * SLOT + 2 * X + 1)
        return pltpu.roll(rim_calc[k, pl.ds(top, 8), :], lax.rem(shift, CZ), 1)

    def weigh(X):
        for t in range(TILES):
            top = 7 + 8 * t
            rows = slice(top, top + 8)
            total = total_v[X, rows, :]
            here = (total & 255).astype(jnp.float32)
            up = ((total >> 8) & 255).astype(jnp.float32)
            down = (total >> 16).astype(jnp.float32)
            edge = at_edges(0, 0, X, top)
            inv = 1.0 / (here + jnp.where(first, edge, roll_lanes(up, 1)) + jnp.where(final, edge, roll_lanes(down, -1)))
            inv_v[X, rows, :] = inv
            w = uv[0, X, rows, :] * inv
            for q in range(6):
                value = w if q == 0 else w * uv[q, X, rows, :]
                k, slot = (2, 2) if q == 0 else (1 + (q - 1) // 3, (q - 1) % 3)
                edge = at_edges(k, slot, X, top)
                w_v[q, X, rows, :] = value
                up_v[q, X, rows, :] = value + jnp.where(final, edge, roll_lanes(value, -1))
                down_v[q, X, rows, :] = value + jnp.where(first, edge, roll_lanes(value, 1))

    def gather(start, slabs, t):
        top = 7 + 8 * t
        rows = pl.ds(top, 8)

        def step(X, behind, here, ahead):
            targets = []
            for dx, use in ((1, behind), (0, here), (-1, ahead)):
                if use is not None:
                    y, z = y_v[X - dx, rows, :], z_v[X - dx, rows, :]
                    along = None if dx == 0 else towards(xy_v[X - dx, rows, :], None, dx, 0)
                    targets.append((dx, along, y == 2.0, y == 0.0, z == 2.0, z == 0.0))
            new = {dx: [] for dx, *_ in targets}
            for q in range(6):
                lines = [[ref[q, X, pl.ds(top + dy, 8), :] for ref in (up_v, down_v, w_v)] for dy in (-1, 0, 1)]
                for dx, along, y_up, y_down, z_up, z_down in targets:
                    low, mid, high = (jnp.where(z_up, a, jnp.where(z_down, b, c)) for a, b, c in lines)
                    plane = mid + jnp.where(y_up, high, jnp.where(y_down, low, 0.0))
                    if along is not None:
                        plane = jnp.where(along, plane, 0.0)
                    old = {1: behind, 0: here, -1: ahead}[dx][q]
                    new[dx].append(plane if old is None else old + plane)
            return new

        none = [None] * 6
        one = step(start - 1, None, None, none)[-1]
        both = step(start, None, one, none)

        def walk(X, sums):
            new = step(X, list(sums[:6]), list(sums[6:]), none)
            inv = 1.0 / new[1][0]
            for q in range(5):
                avg_v[q, X - 1, rows, :] = new[1][q + 1] * inv
            return (*new[0], *new[-1])

        lax.fori_loop(start + 1, start + slabs + 1, walk, (*both[0], *both[-1]))

    def scatter(X):
        for t in range(4):
            top = 8 + 8 * t
            here, up, down = [None] * 5, [None] * 5, [None] * 5
            for dx, dy in SIGNS:
                at = slice(top - dy, top - dy + 8)
                if (dx, dy) == (0, 0):
                    z = z_v[X, at, :]
                    hit, z_up, z_down = None, z == 2.0, z == 0.0
                else:
                    signs = (y_v if dx == 0 else xy_v)[X - dx, at, :]
                    hit = towards(signs, signs, dx, dy)
                    z = (code if dx * dy else yz_v if dx == 0 else xz_v)[X - dx, at, :]
                    full = 9 * (dx + 1) + 3 * (dy + 1) if dx * dy else 3 * (dx + dy + 1)
                    z_up, z_down = z == full + 2.0, z == full + 0.0
                for q in range(5):
                    a = avg_v[q, X - dx, at, :]
                    terms = (a if hit is None else jnp.where(hit, a, 0.0), jnp.where(z_up, a, 0.0), jnp.where(z_down, a, 0.0))
                    here[q], up[q], down[q] = (
                        new if old is None else old + new for old, new in zip((here[q], up[q], down[q]), terms))
            inv = inv_v[X, top:top + 8, :]
            for q in range(5):
                edge = at_edges(3 + q // 3, q % 3, X, top)
                total = here[q] + jnp.where(first, edge, roll_lanes(up[q], 1)) + jnp.where(
                    final, edge, roll_lanes(down[q], -1))
                out_ref[q, X - 2, 8 * t:8 * t + 8, :] = total * inv

    def loop(lo, hi, body):
        def step(k, _):
            body(k)
            return _

        lax.fori_loop(lo, hi, step, 0)

    def both_ends(k, low, high):
        return k + low + (k // 2) * (high - low - 2)

    def unpack_y(X, fields):
        for s, near, far in ((0, 7, 6), (1, 40, 41)):
            code[X, near:near + 1, :] = y_recv[s, X, 6:7, :]
            code[X, far:far + 1, :] = y_recv[s, X, 7:8, :]
            if fields:
                for q in range(6):
                    uv[q, X, near:near + 1, :] = y_recv[s, X, q:q + 1, :]

    lane = lanes_of((ROWS, CZ))

    def planes(own, from_lower, from_upper):
        ghost = [jnp.where(lane % 2 == 1, roll_lanes(a, 1), roll_lanes(b, -1)) for a, b in zip(from_lower, from_upper)]
        entering, ghost_w, deposits = rim_planes(own, ghost, lane)
        for k, a in enumerate((entering, *ghost_w, *deposits)):
            rim_calc[k] = a

    def own_signs(X):
        for t in range(4):
            write_signs(X, 8 + 8 * t)

    loop(2, 18, own_signs)
    loop(3, 17, lambda X: count(X, (1, 2, 3)))

    for s in (0, 1):
        @when(has_y[s])
        def _(s=s):
            y_copies(1 - s, 0)[0].wait_recv()
    for i in (0, 1):
        @when(has_x[i])
        def _(i=i):
            d_copy(i).start()

    def y_ghosts(X):
        unpack_y(X, True)

    loop(2, 18, y_ghosts)

    def ghost_signs(X):
        write_signs(X, 0)
        write_signs(X, 40)

    loop(2, 18, ghost_signs)
    loop(3, 17, lambda X: count(X, (0, 4)))

    for s in (0, 1):
        @when(has_y[s])
        def _(s=s):
            y_copies(1 - s, 1)[0].wait_recv()

        @when(has_z[s])
        def _(s=s):
            z_copy(1 - s).wait_recv()

        for j in (0, 1):
            @when(has_yz[j][s])
            def _(s=s, j=j):
                yz_copy(1 - j, 1 - s).wait_recv()
    planes([rim_own[b] for b in range(3)], [rim_ghost[0, b] for b in range(3)], [rim_ghost[1, b] for b in range(3)])

    loop(3, 17, weigh)
    loop(0, TILES, lambda t: gather(3, 14, t))

    for s in (0, 1):
        @when(has_x[s])
        def _(s=s):
            for copy in x_copies(1 - s):
                copy.wait_recv()
            d_copy(1 - s).wait_recv()

    loop(0, 2, lambda k: unpack_y(1 + 17 * k, True))
    loop(0, 2, lambda k: unpack_y(19 * k, False))
    loop(0, TILES, lambda t: pack_rims(rim_x, (0, 1, 18, 19), 6 + 8 * t))
    for i in (0, 1):
        @when(has_z[i])
        def _(i=i):
            zx_copy(i).start()

    def end_signs(k):
        for t in range(6):
            write_signs(both_ends(k, 0, 18), 8 * t)

    loop(0, 4, end_signs)
    loop(0, 4, lambda k: count(both_ends(k, 1, 17), range(TILES)))
    loop(4, 16, scatter)
    for s in (0, 1):
        @when(has_z[s])
        def _(s=s):
            zx_copy(1 - s).wait_recv()
    place = lane % SLOT
    at_x = (place < 4) | (place >= 36)

    def with_x(rim, rim_of_x):
        return [jnp.where(at_x, rim_of_x[b], rim[b]) for b in range(3)]

    planes(with_x(rim_own, rim_x), *(with_x(rim_ghost.at[s], rim_ghost_x.at[s]) for s in (0, 1)))
    loop(0, 4, lambda k: weigh(both_ends(k, 1, 17)))
    loop(0, 2 * TILES, lambda k: gather(1 + 15 * (k // TILES), 3, k % TILES))
    loop(0, 4, lambda k: scatter(both_ends(k, 2, 16)))

    for i in (0, 1):
        @when(has_x[i])
        def _(i=i):
            for copy in (*x_copies(i), d_copy(i)):
                copy.wait_send()

        @when(has_y[i])
        def _(i=i):
            for copy in y_copies(i):
                copy.wait_send()

        @when(has_z[i])
        def _(i=i):
            z_copy(i).wait_send()
            zx_copy(i).wait_send()

        for j in (0, 1):
            @when(has_yz[j][i])
            def _(i=i, j=j):
                yz_copy(j, i).wait_send()


def solution(mesh, nby=NBY, nbz=NBZ):
    nbx = mesh.shape["boxes"] // (nby * nbz)
    f32 = jnp.float32

    def per_device(*args):
        dma = pltpu.SemaphoreType.DMA
        extended = pltpu.VMEM((21, ROWS, CZ), f32)
        values = pltpu.VMEM((6, 21, ROWS, CZ), f32)
        out = pl.pallas_call(
            functools.partial(kernel, (nbx, nby, nbz)),
            out_shape=jax.ShapeDtypeStruct((5, CX, CY, CZ), f32),
            in_specs=[pl.BlockSpec(memory_space=pltpu.HBM)] * 4,
            out_specs=pl.BlockSpec(memory_space=pltpu.VMEM),
            scratch_shapes=[
                values,
                extended, extended, extended, extended, extended, extended,
                pltpu.VMEM((21, ROWS, CZ), jnp.int32),
                pltpu.VMEM((21, ROWS, CZ), jnp.int32),
                pltpu.VMEM((CX, CY, CZ), jnp.int32),
                pltpu.VMEM((CX, CY, CZ), jnp.int32),
                pltpu.VMEM((2, CX, 8, CZ), f32),
                pltpu.VMEM((2, 20, 8, CZ), f32),
                pltpu.VMEM((3, ROWS, CZ), f32),
                pltpu.VMEM((2, 3, ROWS, CZ), f32),
                pltpu.VMEM((3, ROWS, CZ), f32),
                pltpu.VMEM((2, 3, ROWS, CZ), f32),
                pltpu.VMEM((5, ROWS, CZ), f32),
                values, values, values,
                extended,
                values,
                dma((4,)), dma((2, 2)), dma((2, 2)), dma((2, 2)), dma((2, 2)), dma((2,)), dma((2,)), dma((2,)), dma((2,)),
                dma((2, 2)), dma((2, 2)), dma((2,)), dma((2,)),
            ],
            compiler_params=pltpu.CompilerParams(
                collective_id=0, has_side_effects=True, vmem_limit_bytes=30 * 1024 * 1024
            ),
        )(*(pltpu.with_memory_space_constraint(a[0], pltpu.HBM) for a in args))
        return out[None]

    return jax.shard_map(
        per_device,
        mesh=mesh,
        in_specs=(
            P("boxes", None, None, None, None),
            P("boxes", None, None, None),
            P("boxes", None, None, None),
            P("boxes", None, None, None),
        ),
        out_specs=P("boxes", None, None, None, None),
        check_vma=False,
    )
```

time: 260 us -> 30.1 us (0.12)
  the two profiles are of different devices: /device:TPU:129 before, /device:TPU:35 now
where the time goes in v2:
time: 30.1 us; the launch traced here: 30 us
  Pallas kernels  29 us (96%)
  local copies, waits for them, and re-layouts  1.06 us (4%)
    pallas_call x1, Pallas kernels, per_device(): pl.pallas_call(functools.partial(kernel, (nbx, nby, nbz)), out_shape=jax....  29 us
    unnamed x1, local copies, waits for them, and re-layouts  1.06 us

profile of v2, /device:TPU:35, one launch (start us, length us, event | category | flops | bytes accessed | tf_op | source)
XLA Modules:
  0.0 30.0 jit_solution(13390584600733600341)
XLA Ops:
  0.0 29.0 %shard_map.46 = f32[5,16,32,128]{3,2,1,0:T(8,128)S(1)} custom-call(f32[5,16,32,128]{3,2,1,0:T(8,128)} %bitcast.6, f32[16,32,128]{2,1,0:T(8,128)} %bitcast.7, s32[16,32,128]{2,1,0:T(8,128)} %bitcast.8, s32[16,32,128]{2,1,0:T(8,128)} %bitcast.9), custom_call_target="tpu_custom_call" | custom-call | tf_op jit(solution)/shard_map/pallas_call | solution.py:544
  29.0 1.1 %copy.6 = f32[1,5,16,32,128]{4,3,2,1,0:T(8,128)} copy(f32[1,5,16,32,128]{4,3,2,1,0:T(8,128)S(1)} %bitcast.5) | data formatting | bytes 2621440

commit v3 on v2

--- a/solution.py
+++ b/solution.py
@@ -113,10 +113,10 @@
 
 def kernel(
     sizes, u_hbm, vf_hbm, mask_hbm, code_hbm, out_ref,
-    uv, code, xy_v, y_v, z_v, xz_v, yz_v, ones_v, total_v, mask_raw, code_raw, y_send, y_recv, rim_own, rim_ghost, rim_x,
-    rim_ghost_x, rim_calc, w_v, up_v, down_v, inv_v, avg_v,
+    uv, code, xy_v, y_v, z_v, xz_v, yz_v, ones_v, total_v, mask_raw, code_raw, y_send, y_recv, rim_own, rim_ghost, edge_send,
+    edge_own, edge_ghost, rim_calc, w_v, up_v, down_v, inv_v, avg_v,
     load_sem, x_send_sem, x_recv_sem, y_send_sem, y_recv_sem, d_send_sem, d_recv_sem, z_send_sem, z_recv_sem,
-    yz_send_sem, yz_recv_sem, zx_send_sem, zx_recv_sem,
+    yz_send_sem, yz_recv_sem, ex_send_sem, ex_recv_sem, ey_send_sem, ey_recv_sem, ez_send_sem, ez_recv_sem,
 ):
     nbx, nby, nbz = sizes
     me = lax.axis_index("boxes")
@@ -176,20 +176,29 @@
         return [
             remote(y_send.at[i], y_recv.at[1 - i, 2:18], y_send_sem.at[i, 0], y_recv_sem.at[1 - i, 0], steps[i] * y_step),
         ] * (which != 1) + [
-            remote(rim_own.at[:, pl.ds(rim_src[i], 8)], rim_own.at[:, pl.ds(rim_dst[i], 8)], y_send_sem.at[i, 1],
+            remote(rim_own.at[0:3, pl.ds(rim_src[i], 8)], rim_own.at[0:3, pl.ds(rim_dst[i], 8)], y_send_sem.at[i, 1],
                    y_recv_sem.at[1 - i, 1], steps[i] * y_step),
         ] * (which != 0)
 
     def z_copy(i):
-        return remote(rim_own.at[:, 8:40], rim_ghost.at[1 - i, :, 8:40], z_send_sem.at[i], z_recv_sem.at[1 - i], steps[i])
+        return remote(rim_own.at[0:3, 8:40], rim_ghost.at[1 - i, 0:3, 8:40], z_send_sem.at[i], z_recv_sem.at[1 - i], steps[i])
 
     def yz_copy(j, i):
         return remote(
-            rim_own.at[:, pl.ds(rim_src[j], 8)], rim_ghost.at[1 - i, :, pl.ds(rim_dst[j], 8)], yz_send_sem.at[j, i],
+            rim_own.at[0:3, pl.ds(rim_src[j], 8)], rim_ghost.at[1 - i, 0:3, pl.ds(rim_dst[j], 8)], yz_send_sem.at[j, i],
             yz_recv_sem.at[1 - j, 1 - i], steps[j] * y_step + steps[i])
 
-    def zx_copy(i):
-        return remote(rim_x, rim_ghost_x.at[1 - i], zx_send_sem.at[i], zx_recv_sem.at[1 - i], steps[i])
+    def ex_copy(i):
+        return remote(edge_send, edge_own.at[1 - i, 8:40], ex_send_sem.at[i], ex_recv_sem.at[1 - i], steps[i] * x_step)
+
+    def ey_copy(i):
+        return remote(edge_own.at[:, pl.ds(rim_src[i], 8)], edge_own.at[:, pl.ds(rim_dst[i], 8)], ey_send_sem.at[i],
+                      ey_recv_sem.at[1 - i], steps[i] * y_step)
+
+    def ez_copy(i, part):
+        rows = pl.ds((8, 0, 40)[part], (32, 8, 8)[part])
+        return remote(edge_own.at[:, rows], edge_ghost.at[1 - i, :, rows], ez_send_sem.at[i, part],
+                      ez_recv_sem.at[1 - i, part], steps[i])
 
     loads[0].wait()
     loads[1].wait()
@@ -247,17 +256,28 @@
         return _
 
     lax.fori_loop(0, 4, pack_own_rims, 0)
+
+    lane32 = lanes_of((CY, CZ))
+    kept = ((lane32 % SLOT) // 4 == 1) | ((lane32 % SLOT) // 4 == 8)
+    compact = jnp.zeros((CY, CZ), jnp.float32)
+    for b in range(3):
+        compact = compact + roll_lanes(jnp.where(kept & (lane32 < (2 if b == 2 else 3) * SLOT), rim_own[b, 8:40, :], 0.0), 8 * b)
+    edge_send[...] = compact
     pl.semaphore_wait(barrier, greeted)
 
+    for i in (0, 1):
+        @when(has_z[i])
+        def _(i=i):
+            z_copy(i).start()
+    for i in (0, 1):
+        @when(has_x[i])
+        def _(i=i):
+            ex_copy(i).start()
     for i in (0, 1):
         @when(has_y[i])
         def _(i=i):
             for copy in y_copies(i):
                 copy.start()
-
-        @when(has_z[i])
-        def _(i=i):
-            z_copy(i).start()
 
         for j in (0, 1):
             @when(has_yz[j][i])
@@ -275,9 +295,16 @@
         for b in range(3):
             rim[b, first:first + rows, :] = jnp.full((rows, CZ), 13.0 if b == 2 else 0.0, jnp.float32)
 
+    def blank_edge(rows):
+        spot = lanes_of((rows, CZ)) - 16
+        is_code = (spot >= 0) & (spot < 2 * SLOT) & (((spot % SLOT) // 4 == 1) | ((spot % SLOT) // 4 == 8))
+        return jnp.where(is_code, 13.0, 0.0)
+
     for s in (0, 1):
         @when(jnp.logical_not(has_y[s]))
         def _(s=s):
+            for side in (0, 1):
+                edge_own[side, 40 * s:40 * s + 8, :] = blank_edge(8)
             blank_rim(rim_own, 0 if s == 0 else 40, 8)
             for X in range(2, 18):
                 y_recv[s, X] = jnp.where(tile_row < 6, 0.0, 13.0)
@@ -285,7 +312,8 @@
         @when(jnp.logical_not(has_z[s]))
         def _(s=s):
             blank_rim(rim_ghost.at[s], 8, 32)
-            blank_rim(rim_ghost_x.at[s], 0, ROWS)
+            for side in (0, 1):
+                edge_ghost[s, side] = blank_edge(ROWS)
 
         for j in (0, 1):
             @when(jnp.logical_not(has_yz[j][s]))
@@ -295,6 +323,7 @@
         @when(jnp.logical_not(has_x[s]))
         def _(s=s):
             u_at, c_at = (1, 0) if s == 0 else (18, 18)
+            edge_own[s, 8:40, :] = blank_edge(CY)
             for q in range(6):
                 uv[q, u_at, 8:40, :] = jnp.zeros((CY, CZ), jnp.float32)
             for c in (0, 1):
@@ -319,10 +348,10 @@
         shift = CZ * 2 - (slot * SLOT + 2 * X + 1)
         return pltpu.roll(rim_calc[k, pl.ds(top, 8), :], lax.rem(shift, CZ), 1)
 
-    def weigh(X):
-        for t in range(TILES):
+    def weigh(X, tiles=range(TILES)):
+        for t in tiles:
             top = 7 + 8 * t
-            rows = slice(top, top + 8)
+            rows = pl.ds(top, 8)
             total = total_v[X, rows, :]
             here = (total & 255).astype(jnp.float32)
             up = ((total >> 8) & 255).astype(jnp.float32)
@@ -336,8 +365,8 @@
                 k, slot = (2, 2) if q == 0 else (1 + (q - 1) // 3, (q - 1) % 3)
                 edge = at_edges(k, slot, X, top)
                 w_v[q, X, rows, :] = value
-                up_v[q, X, rows, :] = value + jnp.where(final, edge, roll_lanes(value, -1))
-                down_v[q, X, rows, :] = value + jnp.where(first, edge, roll_lanes(value, 1))
+                up_v[q, X, pl.ds(top + 8, 8), :] = value + jnp.where(final, edge, roll_lanes(value, -1))
+                down_v[q, X, pl.ds(top + 16, 8), :] = value + jnp.where(first, edge, roll_lanes(value, 1))
 
     def gather(start, slabs, t):
         top = 7 + 8 * t
@@ -352,7 +381,7 @@
                     targets.append((dx, along, y == 2.0, y == 0.0, z == 2.0, z == 0.0))
             new = {dx: [] for dx, *_ in targets}
             for q in range(6):
-                lines = [[ref[q, X, pl.ds(top + dy, 8), :] for ref in (up_v, down_v, w_v)] for dy in (-1, 0, 1)]
+                lines = [[ref[q, X, pl.ds(top + dy + shift, 8), :] for ref, shift in ((up_v, 8), (down_v, 16), (w_v, 0))] for dy in (-1, 0, 1)]
                 for dx, along, y_up, y_down, z_up, z_down in targets:
                     low, mid, high = (jnp.where(z_up, a, jnp.where(z_down, b, c)) for a, b, c in lines)
                     plane = mid + jnp.where(y_up, high, jnp.where(y_down, low, 0.0))
@@ -375,12 +404,12 @@
 
         lax.fori_loop(start + 1, start + slabs + 1, walk, (*both[0], *both[-1]))
 
-    def scatter(X):
-        for t in range(4):
+    def scatter(X, tiles=range(4)):
+        for t in tiles:
             top = 8 + 8 * t
             here, up, down = [None] * 5, [None] * 5, [None] * 5
             for dx, dy in SIGNS:
-                at = slice(top - dy, top - dy + 8)
+                at = pl.ds(top - dy, 8)
                 if (dx, dy) == (0, 0):
                     z = z_v[X, at, :]
                     hit, z_up, z_down = None, z == 2.0, z == 0.0
@@ -395,12 +424,12 @@
                     terms = (a if hit is None else jnp.where(hit, a, 0.0), jnp.where(z_up, a, 0.0), jnp.where(z_down, a, 0.0))
                     here[q], up[q], down[q] = (
                         new if old is None else old + new for old, new in zip((here[q], up[q], down[q]), terms))
-            inv = inv_v[X, top:top + 8, :]
+            inv = inv_v[X, pl.ds(top, 8), :]
             for q in range(5):
                 edge = at_edges(3 + q // 3, q % 3, X, top)
                 total = here[q] + jnp.where(first, edge, roll_lanes(up[q], 1)) + jnp.where(
                     final, edge, roll_lanes(down[q], -1))
-                out_ref[q, X - 2, 8 * t:8 * t + 8, :] = total * inv
+                out_ref[q, X - 2, pl.ds(8 * t if isinstance(t, int) else pl.multiple_of(8 * t, 8), 8), :] = total * inv
 
     def loop(lo, hi, body):
         def step(k, _):
@@ -422,11 +451,12 @@
 
     lane = lanes_of((ROWS, CZ))
 
-    def planes(own, from_lower, from_upper):
+    def planes(own, from_lower, from_upper, inner=False):
+        lane = lanes_of(own[0].shape)
         ghost = [jnp.where(lane % 2 == 1, roll_lanes(a, 1), roll_lanes(b, -1)) for a, b in zip(from_lower, from_upper)]
         entering, ghost_w, deposits = rim_planes(own, ghost, lane)
-        for k, a in enumerate((entering, *ghost_w, *deposits)):
-            rim_calc[k] = a
+        for k, a in enumerate((entering, *ghost_w) if inner else (entering, *ghost_w, *deposits)):
+            rim_calc[k, 8 if inner else 0:40 if inner else ROWS, :] = a
 
     def own_signs(X):
         for t in range(4):
@@ -436,6 +466,14 @@
     loop(3, 17, lambda X: count(X, (1, 2, 3)))
 
     for s in (0, 1):
+        @when(has_z[s])
+        def _(s=s):
+            z_copy(1 - s).wait_recv()
+    planes(*([rim[b, 8:40, :] for b in range(3)] for rim in (rim_own, rim_ghost.at[0], rim_ghost.at[1])), inner=True)
+    loop(3, 17, lambda X: weigh(X, (1, 2, 3)))
+    gather(3, 14, 2)
+
+    for s in (0, 1):
         @when(has_y[s])
         def _(s=s):
             y_copies(1 - s, 0)[0].wait_recv()
@@ -457,13 +495,22 @@
     loop(3, 17, lambda X: count(X, (0, 4)))
 
     for s in (0, 1):
+        @when(has_x[s])
+        def _(s=s):
+            ex_copy(1 - s).wait_recv()
+    for i in (0, 1):
+        @when(has_y[i])
+        def _(i=i):
+            ey_copy(i).start()
+
+        @when(has_z[i])
+        def _(i=i):
+            ez_copy(i, 0).start()
+
+    for s in (0, 1):
         @when(has_y[s])
         def _(s=s):
             y_copies(1 - s, 1)[0].wait_recv()
-
-        @when(has_z[s])
-        def _(s=s):
-            z_copy(1 - s).wait_recv()
 
         for j in (0, 1):
             @when(has_yz[j][s])
@@ -471,8 +518,35 @@
                 yz_copy(1 - j, 1 - s).wait_recv()
     planes([rim_own[b] for b in range(3)], [rim_ghost[0, b] for b in range(3)], [rim_ghost[1, b] for b in range(3)])
 
-    loop(3, 17, weigh)
-    loop(0, TILES, lambda t: gather(3, 14, t))
+    loop(3, 17, lambda X: weigh(X, (0, 4)))
+    for s in (0, 1):
+        @when(has_y[s])
+        def _(s=s):
+            ey_copy(1 - s).wait_recv()
+    for i in (0, 1):
+        @when(has_z[i])
+        def _(i=i):
+            ez_copy(i, 1).start()
+            ez_copy(i, 2).start()
+    loop(0, TILES - 1, lambda k: gather(3, 14, k + k // 2))
+    loop(4, 16, scatter)
+
+    for s in (0, 1):
+        @when(has_z[s])
+        def _(s=s):
+            for part in range(3):
+                ez_copy(1 - s, part).wait_recv()
+    place = lane % SLOT
+    at_x = (place < 4) | (place >= 36)
+
+    def with_x(rim, edge):
+        low, high = edge[0], edge[1]
+        return [
+            jnp.where(at_x, jnp.where(place < 4, roll_lanes(low, -(32 + 8 * b)), roll_lanes(high, 32 - 8 * b)), rim[b])
+            for b in range(3)
+        ]
+
+    planes(with_x(rim_own, edge_own), *(with_x(rim_ghost.at[s], edge_ghost.at[s]) for s in (0, 1)))
 
     for s in (0, 1):
         @when(has_x[s])
@@ -483,11 +557,6 @@
 
     loop(0, 2, lambda k: unpack_y(1 + 17 * k, True))
     loop(0, 2, lambda k: unpack_y(19 * k, False))
-    loop(0, TILES, lambda t: pack_rims(rim_x, (0, 1, 18, 19), 6 + 8 * t))
-    for i in (0, 1):
-        @when(has_z[i])
-        def _(i=i):
-            zx_copy(i).start()
 
     def end_signs(k):
         for t in range(6):
@@ -495,18 +564,6 @@
 
     loop(0, 4, end_signs)
     loop(0, 4, lambda k: count(both_ends(k, 1, 17), range(TILES)))
-    loop(4, 16, scatter)
-    for s in (0, 1):
-        @when(has_z[s])
-        def _(s=s):
-            zx_copy(1 - s).wait_recv()
-    place = lane % SLOT
-    at_x = (place < 4) | (place >= 36)
-
-    def with_x(rim, rim_of_x):
-        return [jnp.where(at_x, rim_of_x[b], rim[b]) for b in range(3)]
-
-    planes(with_x(rim_own, rim_x), *(with_x(rim_ghost.at[s], rim_ghost_x.at[s]) for s in (0, 1)))
     loop(0, 4, lambda k: weigh(both_ends(k, 1, 17)))
     loop(0, 2 * TILES, lambda k: gather(1 + 15 * (k // TILES), 3, k % TILES))
     loop(0, 4, lambda k: scatter(both_ends(k, 2, 16)))
@@ -514,18 +571,18 @@
     for i in (0, 1):
         @when(has_x[i])
         def _(i=i):
-            for copy in (*x_copies(i), d_copy(i)):
+            for copy in (*x_copies(i), d_copy(i), ex_copy(i)):
                 copy.wait_send()
 
         @when(has_y[i])
         def _(i=i):
-            for copy in y_copies(i):
+            for copy in (*y_copies(i), ey_copy(i)):
                 copy.wait_send()
 
         @when(has_z[i])
         def _(i=i):
-            z_copy(i).wait_send()
-            zx_copy(i).wait_send()
+            for copy in (z_copy(i), *(ez_copy(i, part) for part in range(3))):
+                copy.wait_send()
 
         for j in (0, 1):
             @when(has_yz[j][i])
@@ -539,8 +596,9 @@
 
     def per_device(*args):
         dma = pltpu.SemaphoreType.DMA
-        extended = pltpu.VMEM((21, ROWS, CZ), f32)
-        values = pltpu.VMEM((6, 21, ROWS, CZ), f32)
+        extended = pltpu.VMEM((22, ROWS, CZ), f32)
+        values = pltpu.VMEM((6, 22, ROWS, CZ), f32)
+        shifted = pltpu.VMEM((6, 22, ROWS + 16, CZ), f32)
         out = pl.pallas_call(
             functools.partial(kernel, (nbx, nby, nbz)),
             out_shape=jax.ShapeDtypeStruct((5, CX, CY, CZ), f32),
@@ -549,22 +607,23 @@
             scratch_shapes=[
                 values,
                 extended, extended, extended, extended, extended, extended,
-                pltpu.VMEM((21, ROWS, CZ), jnp.int32),
-                pltpu.VMEM((21, ROWS, CZ), jnp.int32),
+                pltpu.VMEM((22, ROWS, CZ), jnp.int32),
+                pltpu.VMEM((22, ROWS, CZ), jnp.int32),
                 pltpu.VMEM((CX, CY, CZ), jnp.int32),
                 pltpu.VMEM((CX, CY, CZ), jnp.int32),
                 pltpu.VMEM((2, CX, 8, CZ), f32),
                 pltpu.VMEM((2, 20, 8, CZ), f32),
-                pltpu.VMEM((3, ROWS, CZ), f32),
-                pltpu.VMEM((2, 3, ROWS, CZ), f32),
-                pltpu.VMEM((3, ROWS, CZ), f32),
-                pltpu.VMEM((2, 3, ROWS, CZ), f32),
-                pltpu.VMEM((5, ROWS, CZ), f32),
-                values, values, values,
+                pltpu.VMEM((4, ROWS, CZ), f32),
+                pltpu.VMEM((2, 4, ROWS, CZ), f32),
+                pltpu.VMEM((CY, CZ), f32),
+                pltpu.VMEM((2, ROWS, CZ), f32),
+                pltpu.VMEM((2, 2, ROWS, CZ), f32),
+                pltpu.VMEM((6, ROWS, CZ), f32),
+                shifted, shifted, shifted,
                 extended,
                 values,
                 dma((4,)), dma((2, 2)), dma((2, 2)), dma((2, 2)), dma((2, 2)), dma((2,)), dma((2,)), dma((2,)), dma((2,)),
-                dma((2, 2)), dma((2, 2)), dma((2,)), dma((2,)),
+                dma((2, 2)), dma((2, 2)), dma((2,)), dma((2,)), dma((2,)), dma((2,)), dma((2, 3)), dma((2, 3)),
             ],
             compiler_params=pltpu.CompilerParams(
                 collective_id=0, has_side_effects=True, vmem_limit_bytes=30 * 1024 * 1024

time: 30.1 us -> 28.5 us (0.947)
  the two profiles are of different devices: /device:TPU:35 before, /device:TPU:1 now
where the time goes in v3:
time: 28.5 us; the launch traced here: 28.3 us
  Pallas kernels  27.2 us (95%)
  local copies, waits for them, and re-layouts  1.06 us (4%)
    pallas_call x1, Pallas kernels, per_device(): pl.pallas_call(functools.partial(kernel, (nbx, nby, nbz)), out_shape=jax....  27.2 us
    unnamed x1, local copies, waits for them, and re-layouts  1.06 us

profile of v3, /device:TPU:1, one launch (start us, length us, event | category | flops | bytes accessed | tf_op | source)
XLA Modules:
  0.0 28.3 jit_solution(3743721107226656668)
XLA Ops:
  0.0 27.2 %shard_map.46 = f32[5,16,32,128]{3,2,1,0:T(8,128)S(1)} custom-call(f32[5,16,32,128]{3,2,1,0:T(8,128)} %bitcast.6, f32[16,32,128]{2,1,0:T(8,128)} %bitcast.7, s32[16,32,128]{2,1,0:T(8,128)} %bitcast.8, s32[16,32,128]{2,1,0:T(8,128)} %bitcast.9), custom_call_target="tpu_custom_call" | custom-call | tf_op jit(solution)/shard_map/pallas_call | solution.py:602
  27.2 1.1 %copy.6 = f32[1,5,16,32,128]{4,3,2,1,0:T(8,128)} copy(f32[1,5,16,32,128]{4,3,2,1,0:T(8,128)S(1)} %bitcast.5) | data formatting | bytes 2621440

commit v4 on v3

--- a/solution.py
+++ b/solution.py
@@ -13,6 +13,7 @@
 MESH = pl.DeviceIdType.MESH
 
 ROWS = 48
+SLAB = 64
 SLOT = 40
 SIGNS = [(dx, dy) for dx in (-1, 0, 1) for dy in (-1, 0, 1)]
 
@@ -399,7 +400,7 @@
             new = step(X, list(sums[:6]), list(sums[6:]), none)
             inv = 1.0 / new[1][0]
             for q in range(5):
-                avg_v[q, X - 1, rows, :] = new[1][q + 1] * inv
+                avg_v[q, X - 1, pl.ds(top + 8 * (q % 3), 8), :] = new[1][q + 1] * inv
             return (*new[0], *new[-1])
 
         lax.fori_loop(start + 1, start + slabs + 1, walk, (*both[0], *both[-1]))
@@ -420,7 +421,7 @@
                     full = 9 * (dx + 1) + 3 * (dy + 1) if dx * dy else 3 * (dx + dy + 1)
                     z_up, z_down = z == full + 2.0, z == full + 0.0
                 for q in range(5):
-                    a = avg_v[q, X - dx, at, :]
+                    a = avg_v[q, X - dx, pl.ds(top - dy + 8 * (q % 3), 8), :]
                     terms = (a if hit is None else jnp.where(hit, a, 0.0), jnp.where(z_up, a, 0.0), jnp.where(z_down, a, 0.0))
                     here[q], up[q], down[q] = (
                         new if old is None else old + new for old, new in zip((here[q], up[q], down[q]), terms))
@@ -449,14 +450,15 @@
                 for q in range(6):
                     uv[q, X, near:near + 1, :] = y_recv[s, X, q:q + 1, :]
 
-    lane = lanes_of((ROWS, CZ))
+    near_rows = slice(4, 44)
+    lane = lanes_of((40, CZ))
 
     def planes(own, from_lower, from_upper, inner=False):
         lane = lanes_of(own[0].shape)
         ghost = [jnp.where(lane % 2 == 1, roll_lanes(a, 1), roll_lanes(b, -1)) for a, b in zip(from_lower, from_upper)]
         entering, ghost_w, deposits = rim_planes(own, ghost, lane)
         for k, a in enumerate((entering, *ghost_w) if inner else (entering, *ghost_w, *deposits)):
-            rim_calc[k, 8 if inner else 0:40 if inner else ROWS, :] = a
+            rim_calc[k, slice(8, 40) if inner else near_rows, :] = a
 
     def own_signs(X):
         for t in range(4):
@@ -470,8 +472,8 @@
         def _(s=s):
             z_copy(1 - s).wait_recv()
     planes(*([rim[b, 8:40, :] for b in range(3)] for rim in (rim_own, rim_ghost.at[0], rim_ghost.at[1])), inner=True)
-    loop(3, 17, lambda X: weigh(X, (1, 2, 3)))
-    gather(3, 14, 2)
+    loop(0, 7, lambda k: [weigh(3 + 2 * k + i, (1, 2, 3)) for i in (0, 1)])
+    gather(4, 12, 2)
 
     for s in (0, 1):
         @when(has_y[s])
@@ -516,9 +518,9 @@
             @when(has_yz[j][s])
             def _(s=s, j=j):
                 yz_copy(1 - j, 1 - s).wait_recv()
-    planes([rim_own[b] for b in range(3)], [rim_ghost[0, b] for b in range(3)], [rim_ghost[1, b] for b in range(3)])
-
-    loop(3, 17, lambda X: weigh(X, (0, 4)))
+    planes(*([rim[b, near_rows, :] for b in range(3)] for rim in (rim_own, rim_ghost.at[0], rim_ghost.at[1])))
+
+    loop(0, 7, lambda k: [weigh(3 + 2 * k + i, (0, 4)) for i in (0, 1)])
     for s in (0, 1):
         @when(has_y[s])
         def _(s=s):
@@ -528,8 +530,8 @@
         def _(i=i):
             ez_copy(i, 1).start()
             ez_copy(i, 2).start()
-    loop(0, TILES - 1, lambda k: gather(3, 14, k + k // 2))
-    loop(4, 16, scatter)
+    loop(0, TILES - 1, lambda k: gather(4, 12, k + k // 2))
+    loop(5, 15, scatter)
 
     for s in (0, 1):
         @when(has_z[s])
@@ -540,9 +542,9 @@
     at_x = (place < 4) | (place >= 36)
 
     def with_x(rim, edge):
-        low, high = edge[0], edge[1]
+        low, high = edge[0, near_rows, :], edge[1, near_rows, :]
         return [
-            jnp.where(at_x, jnp.where(place < 4, roll_lanes(low, -(32 + 8 * b)), roll_lanes(high, 32 - 8 * b)), rim[b])
+            jnp.where(at_x, jnp.where(place < 4, roll_lanes(low, -(32 + 8 * b)), roll_lanes(high, 32 - 8 * b)), rim[b, near_rows, :])
             for b in range(3)
         ]
 
@@ -566,7 +568,7 @@
     loop(0, 4, lambda k: count(both_ends(k, 1, 17), range(TILES)))
     loop(0, 4, lambda k: weigh(both_ends(k, 1, 17)))
     loop(0, 2 * TILES, lambda k: gather(1 + 15 * (k // TILES), 3, k % TILES))
-    loop(0, 4, lambda k: scatter(both_ends(k, 2, 16)))
+    loop(0, 6, lambda k: scatter(2 + k + 10 * (k // 3)))
 
     for i in (0, 1):
         @when(has_x[i])
@@ -596,9 +598,8 @@
 
     def per_device(*args):
         dma = pltpu.SemaphoreType.DMA
-        extended = pltpu.VMEM((22, ROWS, CZ), f32)
-        values = pltpu.VMEM((6, 22, ROWS, CZ), f32)
-        shifted = pltpu.VMEM((6, 22, ROWS + 16, CZ), f32)
+        extended = pltpu.VMEM((22, SLAB, CZ), f32)
+        values = pltpu.VMEM((6, 22, SLAB, CZ), f32)
         out = pl.pallas_call(
             functools.partial(kernel, (nbx, nby, nbz)),
             out_shape=jax.ShapeDtypeStruct((5, CX, CY, CZ), f32),
@@ -607,8 +608,8 @@
             scratch_shapes=[
                 values,
                 extended, extended, extended, extended, extended, extended,
-                pltpu.VMEM((22, ROWS, CZ), jnp.int32),
-                pltpu.VMEM((22, ROWS, CZ), jnp.int32),
+                pltpu.VMEM((22, SLAB, CZ), jnp.int32),
+                pltpu.VMEM((22, SLAB, CZ), jnp.int32),
                 pltpu.VMEM((CX, CY, CZ), jnp.int32),
                 pltpu.VMEM((CX, CY, CZ), jnp.int32),
                 pltpu.VMEM((2, CX, 8, CZ), f32),
@@ -619,14 +620,14 @@
                 pltpu.VMEM((2, ROWS, CZ), f32),
                 pltpu.VMEM((2, 2, ROWS, CZ), f32),
                 pltpu.VMEM((6, ROWS, CZ), f32),
-                shifted, shifted, shifted,
+                values, values, values,
                 extended,
                 values,
                 dma((4,)), dma((2, 2)), dma((2, 2)), dma((2, 2)), dma((2, 2)), dma((2,)), dma((2,)), dma((2,)), dma((2,)),
                 dma((2, 2)), dma((2, 2)), dma((2,)), dma((2,)), dma((2,)), dma((2,)), dma((2, 3)), dma((2, 3)),
             ],
             compiler_params=pltpu.CompilerParams(
-                collective_id=0, has_side_effects=True, vmem_limit_bytes=30 * 1024 * 1024
+                collective_id=0, has_side_effects=True, vmem_limit_bytes=38 * 1024 * 1024
             ),
         )(*(pltpu.with_memory_space_constraint(a[0], pltpu.HBM) for a in args))
         return out[None]

time: 28.5 us -> 27.5 us (0.965)
  Pallas kernels: 27.2 us -> 26.3 us
    pallas_call x1, Pallas kernels: 27.2 us -> 26.3 us  [per_device(): pl.pallas_call(functools.partial(kernel, (nbx, nby, nbz)), out_shape=jax....]
where the time goes in v4:
time: 27.5 us; the launch traced here: 27.4 us
  Pallas kernels  26.3 us (96%)
  local copies, waits for them, and re-layouts  1.06 us (4%)
    pallas_call x1, Pallas kernels, per_device(): pl.pallas_call(functools.partial(kernel, (nbx, nby, nbz)), out_shape=jax....  26.3 us
    unnamed x1, local copies, waits for them, and re-layouts  1.06 us

profile of v4, /device:TPU:1, one launch (start us, length us, event | category | flops | bytes accessed | tf_op | source)
XLA Modules:
  0.0 27.4 jit_solution(4951603394537795525)
XLA Ops:
  0.0 26.3 %shard_map.46 = f32[5,16,32,128]{3,2,1,0:T(8,128)S(1)} custom-call(f32[5,16,32,128]{3,2,1,0:T(8,128)} %bitcast.6, f32[16,32,128]{2,1,0:T(8,128)} %bitcast.7, s32[16,32,128]{2,1,0:T(8,128)} %bitcast.8, s32[16,32,128]{2,1,0:T(8,128)} %bitcast.9), custom_call_target="tpu_custom_call" | custom-call | tf_op jit(solution)/shard_map/pallas_call | solution.py:603
  26.3 1.1 %copy.6 = f32[1,5,16,32,128]{4,3,2,1,0:T(8,128)} copy(f32[1,5,16,32,128]{4,3,2,1,0:T(8,128)S(1)} %bitcast.5) | data formatting | bytes 2621440

commit v5 on v4

--- a/solution.py
+++ b/solution.py
@@ -403,7 +403,12 @@
                 avg_v[q, X - 1, pl.ds(top + 8 * (q % 3), 8), :] = new[1][q + 1] * inv
             return (*new[0], *new[-1])
 
-        lax.fori_loop(start + 1, start + slabs + 1, walk, (*both[0], *both[-1]))
+        def walk_on(k, sums):
+            for i in range(3):
+                sums = walk(start + 1 + 3 * k + i, sums)
+            return sums
+
+        lax.fori_loop(0, slabs // 3, walk_on, (*both[0], *both[-1]))
 
     def scatter(X, tiles=range(4)):
         for t in tiles:

time: 27.5 us -> 27 us (0.982)
  Pallas kernels: 26.3 us -> 25.8 us
    pallas_call x1, Pallas kernels: 26.3 us -> 25.8 us  [per_device(): pl.pallas_call(functools.partial(kernel, (nbx, nby, nbz)), out_shape=jax....]
where the time goes in v5:
time: 27 us; the launch traced here: 26.9 us
  Pallas kernels  25.8 us (96%)
  local copies, waits for them, and re-layouts  1.06 us (4%)
    pallas_call x1, Pallas kernels, per_device(): pl.pallas_call(functools.partial(kernel, (nbx, nby, nbz)), out_shape=jax....  25.8 us
    unnamed x1, local copies, waits for them, and re-layouts  1.06 us

profile of v5, /device:TPU:1, one launch (start us, length us, event | category | flops | bytes accessed | tf_op | source)
XLA Modules:
  0.0 26.9 jit_solution(9402455374395619780)
XLA Ops:
  0.0 25.8 %shard_map.46 = f32[5,16,32,128]{3,2,1,0:T(8,128)S(1)} custom-call(f32[5,16,32,128]{3,2,1,0:T(8,128)} %bitcast.6, f32[16,32,128]{2,1,0:T(8,128)} %bitcast.7, s32[16,32,128]{2,1,0:T(8,128)} %bitcast.8, s32[16,32,128]{2,1,0:T(8,128)} %bitcast.9), custom_call_target="tpu_custom_call" | custom-call | tf_op jit(solution)/shard_map/pallas_call | solution.py:608
  25.8 1.1 %copy.6 = f32[1,5,16,32,128]{4,3,2,1,0:T(8,128)} copy(f32[1,5,16,32,128]{4,3,2,1,0:T(8,128)S(1)} %bitcast.5) | data formatting | bytes 2621440

commit v6 on v4

--- a/solution.py
+++ b/solution.py
@@ -403,7 +403,10 @@
                 avg_v[q, X - 1, pl.ds(top + 8 * (q % 3), 8), :] = new[1][q + 1] * inv
             return (*new[0], *new[-1])
 
-        lax.fori_loop(start + 1, start + slabs + 1, walk, (*both[0], *both[-1]))
+        sums = lax.fori_loop(
+            0, slabs // 2, lambda k, sums: walk(start + 2 + 2 * k, walk(start + 1 + 2 * k, sums)), (*both[0], *both[-1]))
+        if slabs % 2:
+            walk(start + slabs, sums)
 
     def scatter(X, tiles=range(4)):
         for t in tiles:

time: 27.5 us -> 27 us (0.982)
  Pallas kernels: 26.3 us -> 25.8 us
    pallas_call x1, Pallas kernels: 26.3 us -> 25.8 us  [per_device(): pl.pallas_call(functools.partial(kernel, (nbx, nby, nbz)), out_shape=jax....]
where the time goes in v6:
time: 27 us; the launch traced here: 26.9 us
  Pallas kernels  25.8 us (96%)
  local copies, waits for them, and re-layouts  1.06 us (4%)
    pallas_call x1, Pallas kernels, per_device(): pl.pallas_call(functools.partial(kernel, (nbx, nby, nbz)), out_shape=jax....  25.8 us
    unnamed x1, local copies, waits for them, and re-layouts  1.06 us

profile of v6, /device:TPU:1, one launch (start us, length us, event | category | flops | bytes accessed | tf_op | source)
XLA Modules:
  0.0 26.9 jit_solution(3787608163549178332)
XLA Ops:
  0.0 25.8 %shard_map.46 = f32[5,16,32,128]{3,2,1,0:T(8,128)S(1)} custom-call(f32[5,16,32,128]{3,2,1,0:T(8,128)} %bitcast.6, f32[16,32,128]{2,1,0:T(8,128)} %bitcast.7, s32[16,32,128]{2,1,0:T(8,128)} %bitcast.8, s32[16,32,128]{2,1,0:T(8,128)} %bitcast.9), custom_call_target="tpu_custom_call" | custom-call | tf_op jit(solution)/shard_map/pallas_call | solution.py:606
  25.8 1.1 %copy.6 = f32[1,5,16,32,128]{4,3,2,1,0:T(8,128)} copy(f32[1,5,16,32,128]{4,3,2,1,0:T(8,128)S(1)} %bitcast.5) | data formatting | bytes 2621440
